TPU v7x, 16 devices: a 4x2x1 block of a 4x4x8 slice. The times are simulated.
16 devices in a mesh: replica: 2 (over y, z), model: 8 (over x, core).
Axes of the slice: x: 4, y: 2, z: 1, core: 2. Of those that a mesh axis runs over, the one named last changes fastest.
The devices are a block of a 4x4x8 slice.
Arguments:
- x: bfloat16 [256, 4096], P('replica'), parts along dimension 0
- cache_len: int32 [256], P('replica'), parts along dimension 0
- w_query: bfloat16 [2, 4096, 4096], P(None, None, 'model')
- w_key: bfloat16 [2, 4096, 128], replicated
- w_value: bfloat16 [2, 4096, 128], replicated
- w_out: bfloat16 [2, 4096, 4096], P(None, 'model')
- k_cache: bfloat16 [2, 256, 2048, 128], P(None, ('replica', 'model')), parts along dimension 1
- v_cache: bfloat16 [2, 256, 2048, 128], P(None, ('replica', 'model')), parts along dimension 1
Outputs:
- output 1: bfloat16 [256, 4096], P('replica'), parts along dimension 0
- output 2: bfloat16 [2, 256, 2048, 128], P(None, ('replica', 'model')), parts along dimension 1
- output 3: bfloat16 [2, 256, 2048, 128], P(None, ('replica', 'model')), parts along dimension 1
There are 2 independent parts. A program takes and returns all parts, laid end to end along the dimension named above; an argument that names none is the same for every part.
All inputs are finite; a program needn't handle non-finite values.
Results may differ from a plain program's by a relative error of at most 0.0044712.
Values are sent between devices in bfloat16 or wider.
A program may use at most 768 MiB of HBM per device.

v0:
```python
import jax
import jax.numpy as jnp
from jax import lax
from jax.sharding import PartitionSpec as P, NamedSharding


def write_token(cache, new_rows, cache_len):
    positions = lax.broadcasted_iota(jnp.int32, (1, cache.shape[1], 1), 1)
    return jnp.where(positions == cache_len[:, None, None], new_rows[:, None, :], cache)


def attend_rows(query, k_layer, v_layer, cache_len):
    seq_len = k_layer.shape[1]
    head_dim = k_layer.shape[2]
    scores = jnp.einsum("bhd,bsd->bhs", query, k_layer, preferred_element_type=jnp.float32) * (head_dim ** -0.5)
    positions = lax.broadcasted_iota(jnp.int32, (1, 1, seq_len), 2)
    scores = jnp.where(positions <= cache_len[:, None, None], scores, -jnp.inf)
    weights = jax.nn.softmax(scores, axis=-1).astype(jnp.bfloat16)
    context = jnp.einsum("bhs,bsd->bhd", weights, v_layer, preferred_element_type=jnp.float32)
    return context.astype(jnp.bfloat16)


def solution(mesh):
    groups = mesh.shape["model"]
    row_axes = ("replica", "model")
    cache_spec = P(None, row_axes, None, None)

    def device_step(x, cache_len, w_query, w_key, w_value, w_out, k_cache, v_cache):
        rows = x.shape[0]
        local_rows = rows // groups
        head_dim = k_cache.shape[-1]
        local_heads = w_query.shape[-1] // head_dim
        first_row = lax.axis_index("model") * local_rows
        my_len = lax.dynamic_slice_in_dim(cache_len, first_row, local_rows)
        hidden = x
        k_layers = []
        v_layers = []
        for layer in range(w_query.shape[0]):
            my_rows = lax.dynamic_slice_in_dim(hidden, first_row, local_rows)
            query = jnp.dot(hidden, w_query[layer], preferred_element_type=jnp.float32).astype(jnp.bfloat16)
            query = query.reshape(rows, local_heads, head_dim)
            k_new = jnp.dot(my_rows, w_key[layer], preferred_element_type=jnp.float32).astype(jnp.bfloat16)
            v_new = jnp.dot(my_rows, w_value[layer], preferred_element_type=jnp.float32).astype(jnp.bfloat16)
            k_layer = write_token(k_cache[layer], k_new, my_len)
            v_layer = write_token(v_cache[layer], v_new, my_len)
            query = lax.all_to_all(query, "model", 0, 1, tiled=True)
            context = attend_rows(query, k_layer, v_layer, my_len)
            context = lax.all_to_all(context, "model", 1, 0, tiled=True)
            part_sum = jnp.dot(context.reshape(rows, local_heads * head_dim), w_out[layer], preferred_element_type=jnp.float32)
            total = lax.psum(part_sum, "model")
            hidden = (hidden.astype(jnp.float32) + total).astype(jnp.bfloat16)
            k_layers.append(k_layer)
            v_layers.append(v_layer)
        return hidden, jnp.stack(k_layers), jnp.stack(v_layers)

    return jax.shard_map(
        device_step,
        mesh=mesh,
        in_specs=(P("replica", None), P("replica"), P(None, None, "model"), P(), P(), P(None, "model", None), cache_spec, cache_spec),
        out_specs=(P("replica", None), cache_spec, cache_spec),
        check_vma=False,
    )
```

profile of v0, /device:TPU:113, one launch (start us, length us, event | category | flops | bytes accessed | tf_op | source)
XLA Modules:
  0.0 248.6 jit_solution(4939298074896540217)
XLA Ops:
  7.2 3.4 %fusion.40 = bf16[128,512]{1,0:T(8,128)(2,1)S(1)} fusion(bf16[128,4096]{1,0:T(8,128)(2,1)} %param.8, bf16[2,4096,512]{2,1,0:T(8,128)(2,1)} %param.10), kind=kOutput, calls=%fused_computation.58 | convolution fusion | flops 536936448 | bytes 5373952 | tf_op jit(solution)/shard_map/dot_general | solution.py:40
  11.3 6.0 %all-to-all-start = ((bf16[128,4,128]{2,1,0:T(4,128)(2,1)}), bf16[128,4,128]{2,1,0:T(4,128)(2,1)S(1)}, u32[]{:S(2)}, u32[]{:S(2)}) async-start(bf16[128,4,128]{2,1,0:T(4,128)(2,1)} %reshape.73), calls=%async_computation | async-start | bytes 262144 | tf_op jit(solution)/shard_map/all_to_all | solution.py:46
  17.3 0.7 dynamic_slice.9
  18.0 1.5 convolution_convert_fusion.3
  19.7 1.2 convolution_convert_fusion.2
  20.8 1.5 all-to-all-done
  22.4 11.1 %fusion.72 = (f32[16,32]{1,0:T(8,128)S(1)}, f32[16,32,2048]{2,1,0:T(8,128)}) fusion(pred[16,2048]{1,0:T(8,128)(4,1)S(1)} %get-tuple-element.9, bf16[16,32,128]{2,1,0:T(8,128)(2,1)S(1)} %bitcast.84, pred[16,2048]{1,0:T(8,128)(4,1)S(1)} %get-tuple-element.10, bf16[2,16,2048,128]{3,2,1,0:T(8,128)(2,1)} %param.14, bf16[16,128]{1,0:T(8,128)(2,1)S(1)} %convolution_convert_fusion.3), kind=kOutput, calls=%fused_computation.92 | convolution fusion | flops 276826112 | bytes 12785664 | tf_op jit(solution)/shard_map/sub | solution.py:18
  33.5 9.8 %fusion.46 = bf16[16,32,128]{2,1,0:T(8,128)(2,1)S(1)} fusion(pred[16,2048]{1,0:T(8,128)(4,1)S(1)} %get-tuple-element.10, bf16[2,16,2048,128]{3,2,1,0:T(8,128)(2,1)} %param.15, bf16[16,128]{1,0:T(8,128)(2,1)S(1)} %convolution_convert_fusion.2, f32[16,32,2048]{2,1,0:T(8,128)} %get-tuple-element.12, f32[16,32]{1,0:T(8,128)S(1)} %get-tuple-element.11), kind=kOutput, calls=%fused_computation.60 | convolution fusion | flops 274792448 | bytes 12752896 | tf_op jit(solution)/shard_map/bhs,bsd->bhd/dot_general | solution.py:19
  43.3 8.6 %all_to_all.66 = bf16[16,32,128]{2,0,1:T(8,128)(2,1)S(1)} all-to-all(bf16[16,32,128]{2,0,1:T(8,128)(2,1)S(1)} %copy.18), channel_id=1, replica_groups=mesh['replica'=2,'model'=8] {'model'}, dimensions={1} | all-to-all | bytes 262144 | tf_op jit(solution)/shard_map/all_to_all | solution.py:48
  52.0 4.2 %fusion.18 = f32[128,4096]{1,0:T(8,128)} fusion(bf16[2,512,4096]{2,1,0:T(8,128)(2,1)} %param.13, bf16[16,8,4,128]{3,2,1,0:T(4,128)(2,1)S(1)} %bitcast.78), kind=kOutput, calls=%fused_computation.28 | convolution fusion | flops 536870912 | bytes 6422528 | tf_op jit(solution)/shard_map/dot_general | solution.py:49
  56.3 55.8 %all-reduce.3.cloned.1.call-done = f32[128,4096]{1,0:T(8,128)} async-done(((f32[128,4096]{1,0:T(8,128)}), f32[128,4096]{1,0:T(8,128)}) %all-reduce.3.cloned.1.call-update) | async-done | bytes 2097168 | tf_op jit(solution)/shard_map/psum | solution.py:50
  112.0 2.1 add_convert_fusion.1
  114.3 2.9 %fusion.43 = bf16[128,512]{1,0:T(8,128)(2,1)S(1)} fusion(bf16[128,4096]{1,0:T(8,128)(2,1)S(1)} %add_convert_fusion.1, bf16[2,4096,512]{2,1,0:T(8,128)(2,1)} %param.10), kind=kOutput, calls=%fused_computation.59 | convolution fusion | flops 536936448 | bytes 5373952 | tf_op jit(solution)/shard_map/dot_general | solution.py:40
  117.9 6.0 %all-to-all-start.2 = ((bf16[128,4,128]{2,1,0:T(4,128)(2,1)}), bf16[128,4,128]{2,1,0:T(4,128)(2,1)S(1)}, u32[]{:S(2)}, u32[]{:S(2)}) async-start(bf16[128,4,128]{2,1,0:T(4,128)(2,1)} %reshape.75), calls=%async_computation.2 | async-start | bytes 262144 | tf_op jit(solution)/shard_map/all_to_all | solution.py:46
  123.9 1.5 convolution_convert_fusion.1
  125.4 3.6 %all-to-all-done.2 = bf16[128,4,128]{2,1,0:T(4,128)(2,1)S(1)} async-done(((bf16[128,4,128]{2,1,0:T(4,128)(2,1)}), bf16[128,4,128]{2,1,0:T(4,128)(2,1)S(1)}, u32[]{:S(2)}, u32[]{:S(2)}) %all-to-all-start.2) | async-done | bytes 131104 | tf_op jit(solution)/shard_map/all_to_all | solution.py:46
  129.1 11.1 %fusion.73 = (f32[16,32]{1,0:T(8,128)S(1)}, f32[16,32,2048]{2,1,0:T(8,128)}) fusion(pred[16,2048]{1,0:T(8,128)(4,1)S(1)} %get-tuple-element.9, bf16[16,32,128]{2,1,0:T(8,128)(2,1)S(1)} %bitcast.85, pred[16,2048]{1,0:T(8,128)(4,1)S(1)} %get-tuple-element.10, bf16[2,16,2048,128]{3,2,1,0:T(8,128)(2,1)} %param.14, bf16[16,128]{1,0:T(8,128)(2,1)S(1)} %convolution_convert_fusion.1), kind=kOutput, calls=%fused_computation.93 | convolution fusion | flops 276826112 | bytes 12785664 | tf_op jit(solution)/shard_map/sub | solution.py:18
  140.2 9.8 %fusion.47 = bf16[16,32,128]{2,1,0:T(8,128)(2,1)S(1)} fusion(pred[16,2048]{1,0:T(8,128)(4,1)S(1)} %get-tuple-element.10, bf16[2,16,2048,128]{3,2,1,0:T(8,128)(2,1)} %param.15, bf16[16,128]{1,0:T(8,128)(2,1)S(1)} %convolution_convert_fusion, f32[16,32,2048]{2,1,0:T(8,128)} %get-tuple-element.14, f32[16,32]{1,0:T(8,128)S(1)} %get-tuple-element.13), kind=kOutput, calls=%fused_computation.61 | convolution fusion | flops 274792448 | bytes 12752896 | tf_op jit(solution)/shard_map/bhs,bsd->bhd/dot_general | solution.py:19
  150.7 4.2 %all-to-all-start.3 = ((bf16[16,32,128]{2,0,1:T(8,128)(2,1)}), bf16[16,32,128]{2,0,1:T(8,128)(2,1)S(1)}, u32[]{:S(2)}, u32[]{:S(2)}) async-start(bf16[16,32,128]{2,0,1:T(8,128)(2,1)} %copy.21), calls=%async_computation.3 | async-start | bytes 262144 | tf_op jit(solution)/shard_map/all_to_all | solution.py:48
  154.9 22.8 %broadcast_select_fusion.1 = (bf16[1,16,2048,128]{3,2,1,0:T(8,128)(2,1)}, bf16[1,16,2048,128]{3,2,1,0:T(8,128)(2,1)}, bf16[1,16,2048,128]{3,2,1,0:T(8,128)(2,1)}, bf16[1,16,2048,128]{3,2,1,0:T(8,128)(2,1)}) fusion(pred[16,2048]{1,0:T(8,128)(4,1)S(1)} %get-tuple-element.10, bf16[2,16,2048,128]{3,2,1,0:T(8,128)(2,1)} %param.15, ...), kind=kLoop, calls=%fused_computation.13 | loop fusion | flops 16777216 | bytes 67158016 | tf_op jit(solution)/shard_map/jit(_where)/select_n | solution.py:9
  177.8 4.3 %fusion.14 = f32[128,4096]{1,0:T(8,128)} fusion(bf16[2,512,4096]{2,1,0:T(8,128)(2,1)} %param.13, bf16[16,8,4,128]{3,2,1,0:T(4,128)(2,1)S(1)} %bitcast.79), kind=kOutput, calls=%fused_computation.24 | convolution fusion | flops 536870912 | bytes 6422528 | tf_op jit(solution)/shard_map/dot_general | solution.py:49
  182.2 22.8 %pad_maximum_fusion = (bf16[2,16,2048,128]{3,2,1,0:T(8,128)(2,1)}, bf16[2,16,2048,128]{3,2,1,0:T(8,128)(2,1)}) fusion(bf16[1,16,2048,128]{3,2,1,0:T(8,128)(2,1)} %get-tuple-element.7, bf16[1,16,2048,128]{3,2,1,0:T(8,128)(2,1)} %get-tuple-element.8, bf16[1,16,2048,128]{3,2,1,0:T(8,128)(2,1)} %get-tuple-element.4, bf16[1,16,2048,128]{3,2,1,0:T(8,128)(2,1)} %get-tuple-element.3), kind=kLoop, calls=%fused_computation.2 | loop fusion | flops 16777216 | bytes 67108864 | tf_op jit(solution)/shard_map/stack | solution.py:54
  204.9 34.0 %all-reduce.5.cloned.1.call-done = f32[128,4096]{1,0:T(8,128)} async-done(((f32[128,4096]{1,0:T(8,128)}), f32[128,4096]{1,0:T(8,128)}) %all-reduce.5.cloned.1.call-update) | async-done | bytes 2097168 | tf_op jit(solution)/shard_map/psum | solution.py:50
  239.0 2.8 %add_convert_fusion = bf16[128,4096]{1,0:T(8,128)(2,1)} fusion(f32[128,4096]{1,0:T(8,128)} %all-reduce.5.cloned.1.call-done, bf16[128,4096]{1,0:T(8,128)(2,1)S(1)} %add_convert_fusion.1), kind=kLoop, calls=%fused_computation.48 | loop fusion | flops 1572864 | bytes 4194304 | tf_op jit(solution)/shard_map/convert_element_type | solution.py:51
  (17 shorter events, 2.8 us)
Async XLA Ops:
  7.2 12.5 %copy-start = (bf16[2,4096,128]{2,1,0:T(8,128)(2,1)S(1)}, bf16[2,4096,128]{2,1,0:T(8,128)(2,1)}, u32[]{:S(2)}) copy-start(bf16[2,4096,128]{2,1,0:T(8,128)(2,1)} %param.12) | copy-start | bytes 6291460
  11.3 11.0 %all-to-all-start = ((bf16[128,4,128]{2,1,0:T(4,128)(2,1)}), bf16[128,4,128]{2,1,0:T(4,128)(2,1)S(1)}, u32[]{:S(2)}, u32[]{:S(2)}) async-start(bf16[128,4,128]{2,1,0:T(4,128)(2,1)} %reshape.73), calls=%async_computation | async-start | bytes 262144 | tf_op jit(solution)/shard_map/all_to_all | solution.py:46
  17.3 94.7 %all-reduce.3.cloned.1.call-start = ((), (), s32[]{:S(2)}) async-start(), calls=%async_computation.4 | async-start | bytes 4194304 | tf_op jit(solution)/shard_map/psum | solution.py:50
  117.9 11.1 %all-to-all-start.2 = ((bf16[128,4,128]{2,1,0:T(4,128)(2,1)}), bf16[128,4,128]{2,1,0:T(4,128)(2,1)S(1)}, u32[]{:S(2)}, u32[]{:S(2)}) async-start(bf16[128,4,128]{2,1,0:T(4,128)(2,1)} %reshape.75), calls=%async_computation.2 | async-start | bytes 262144 | tf_op jit(solution)/shard_map/all_to_all | solution.py:46
  150.7 27.0 %all-to-all-start.3 = ((bf16[16,32,128]{2,0,1:T(8,128)(2,1)}), bf16[16,32,128]{2,0,1:T(8,128)(2,1)S(1)}, u32[]{:S(2)}, u32[]{:S(2)}) async-start(bf16[16,32,128]{2,0,1:T(8,128)(2,1)} %copy.21), calls=%async_computation.3 | async-start | bytes 262144 | tf_op jit(solution)/shard_map/all_to_all | solution.py:48
  154.9 84.1 %all-reduce.5.cloned.1.call-start = ((), (), s32[]{:S(2)}) async-start(), calls=%async_computation.5 | async-start | bytes 4194304 | tf_op jit(solution)/shard_map/psum | solution.py:50
Sparse Core Ops, SparseCore 0:
  56.4 55.5 all-reduce.2
  182.3 56.6 all-reduce.4
where the time goes:
time: 252 us; the launch traced here: 249 us
  waiting for transfers between devices  95 us (38%)
  matrix products  61 us (24%)
  other arithmetic  50.6 us (20%)
  starting transfers between devices  16.2 us (6%)
  between operations  14.2 us (6%)
  blocking collectives  8.57 us (3%)
  local copies, waits for them, and re-layouts  3.08 us (1%)
    psum x2, waiting for transfers between devices, device_step(): total = lax.psum(part_sum, 'model')  89.8 us
    select_n x1, other arithmetic, write_token(): jnp.where(positions == cache_len[:, None, None], new_rows[:, None, :], ca...  22.8 us
    another operation x1, other arithmetic, device_step(): return (hidden, jnp.stack(k_layers), jnp.stack(v_layers))  22.8 us
    sub x2, matrix products, attend_rows(): weights = jax.nn.softmax(scores, axis=-1).astype(jnp.bfloat16)  22.3 us
    dot_general x2, matrix products, attend_rows(): jnp.einsum('bhs,bsd->bhd', weights, v_layer, preferred_element_type=jnp.f...  19.6 us
    all_to_all x2, starting transfers between devices, device_step(): query = lax.all_to_all(query, 'model', 0, 1, tiled=True)  12 us
    all_to_all x1, blocking collectives, device_step(): context = lax.all_to_all(context, 'model', 1, 0, tiled=True)  8.57 us
    dot_general x2, matrix products, device_step(): jnp.dot(context.reshape(rows, local_heads * head_dim), w_out[layer], pref...  8.5 us
  transfers between devices with their start and end apart: 5, of which 4 were waited for; matrix products, arithmetic and copies ran while one was open for 20% of the time, Pallas kernels for 0%

commit v1 on v0

v1 whole, which is shorter than its diff:
```python
import functools

import jax
import jax.numpy as jnp
from jax import lax
from jax.experimental import pallas as pl
from jax.experimental.pallas import tpu as pltpu
from jax.sharding import PartitionSpec as P

MESH = pl.DeviceIdType.MESH
F32 = jnp.float32
BF16 = jnp.bfloat16
CHIPS = 4
CHUNKS = 4
MIB = 1 << 20

ANY_SPEC = pl.BlockSpec(memory_space=pltpu.HBM)
VMEM_SPEC = pl.BlockSpec(memory_space=pltpu.VMEM)
SMEM_SPEC = pl.BlockSpec(memory_space=pltpu.SMEM)


def to_hbm(value):
    return pltpu.with_memory_space_constraint(value, pltpu.HBM)


def to_vmem(value):
    return pltpu.with_memory_space_constraint(value, pltpu.VMEM)


def aligned(index, size):
    return pl.ds(pl.multiple_of(index * size, size), size)


class Place:
    def __init__(self, count):
        self.count = count
        self.me = lax.axis_index("model")
        self.chip = self.me // 2
        self.core = self.me % 2
        self.right = (self.chip + 1) % CHIPS
        self.left = (self.chip + CHIPS - 1) % CHIPS
        self.across = (self.chip + 2) % CHIPS
        self.to_right = self.right * 2 + self.core
        self.to_left = self.left * 2 + self.core
        self.sibling = self.chip * 2 + (1 - self.core)

    def peer(self, offset):
        return (self.me + offset) % self.count

    def origin(self, offset):
        return (self.me + self.count - offset) % self.count


def remote(src, dst, send_sem, recv_sem, device):
    return pltpu.make_async_remote_copy(
        src_ref=src, dst_ref=dst, send_sem=send_sem, recv_sem=recv_sem,
        device_id={"model": device}, device_id_type=MESH)


def signal_all(place):
    barrier = pltpu.get_barrier_semaphore()
    for offset in range(1, place.count):
        pl.semaphore_signal(barrier, inc=1, device_id={"model": place.peer(offset)}, device_id_type=MESH)


def wait_all(place):
    pl.semaphore_wait(pltpu.get_barrier_semaphore(), place.count - 1)


def weight_copies(layer, wq, wk, wv, wq_buf, wkv_buf, sems):
    pieces = sems.shape[0] - 2
    depth = wq_buf.shape[0] // pieces
    head_dim = wk.shape[-1]
    copies = [
        pltpu.make_async_copy(wq.at[layer, pl.ds(i * depth, depth), :], wq_buf.at[pl.ds(i * depth, depth), :], sems.at[i])
        for i in range(pieces)
    ]
    copies.append(pltpu.make_async_copy(wk.at[layer], wkv_buf.at[:, pl.ds(0, head_dim)], sems.at[pieces]))
    copies.append(pltpu.make_async_copy(wv.at[layer], wkv_buf.at[:, pl.ds(head_dim, head_dim)], sems.at[pieces + 1]))
    return copies


def add_query(piece, first, hidden, wq_buf, q_acc):
    depth = hidden.shape[-1]
    part = jnp.dot(hidden[piece], wq_buf[aligned(piece, depth), :], preferred_element_type=F32)
    q_acc[...] = part if first else q_acc[...] + part


def new_rows(place, hidden, wkv_buf, kv_new):
    pieces, rows, depth = hidden.shape
    local_rows = rows // place.count
    total = None
    for piece in range(pieces):
        mine = hidden[piece, aligned(place.me, local_rows), :]
        part = jnp.dot(mine, wkv_buf[pl.ds(piece * depth, depth), :], preferred_element_type=F32)
        total = part if total is None else total + part
    kv_new[...] = total.astype(BF16).astype(F32)


def query_copies(place, q_send, q_out, send_sems, recv_sems, incoming):
    heads = q_send.shape[0]
    local_rows = q_out.shape[1]
    copies = []
    for offset in range(1, place.count):
        source = place.origin(offset) if incoming else place.me
        target = place.peer(offset)
        copies.append(remote(
            q_send.at[:, aligned(target, local_rows), :], q_out.at[pl.ds(source * heads, heads)],
            send_sems.at[offset], recv_sems.at[offset], target))
    return copies


def send_order(count):
    return sorted(range(1, count), key=lambda offset: -min(offset, count - offset))


def exchange_query(place, q_acc, q_send, q_out, send_sems, recv_sems):
    heads, rows, head_dim = q_send.shape
    local_rows = q_out.shape[1]
    for head in range(heads):
        q_send[head] = q_acc[:, head * head_dim:(head + 1) * head_dim].astype(BF16)
    outgoing = query_copies(place, q_send, q_out, send_sems, recv_sems, False)
    for offset in send_order(place.count):
        outgoing[offset - 1].start()
    q_out[pl.ds(place.me * heads, heads)] = q_send[:, aligned(place.me, local_rows), :]
    return outgoing


def first_kernel(count, x, wq, wk, wv, k_cache, v_cache,
                 q_out, kv_new, residual, k_vmem, v_vmem,
                 hidden, wq_buf, wkv_buf, q_acc, q_send,
                 x_sems, w_sems, cache_sems, q_ssem, q_rsem):
    place = Place(count)
    pieces, rows, depth = hidden.shape
    x_copies = [
        pltpu.make_async_copy(x.at[:, pl.ds(i * depth, depth)], hidden.at[i], x_sems.at[i]) for i in range(pieces)
    ]
    w_copies = weight_copies(0, wq, wk, wv, wq_buf, wkv_buf, w_sems)
    cache_copies = [
        pltpu.make_async_copy(k_cache.at[0], k_vmem, cache_sems.at[0]),
        pltpu.make_async_copy(v_cache.at[0], v_vmem, cache_sems.at[1]),
    ]
    for i in range(pieces):
        x_copies[i].start()
        w_copies[i].start()
    w_copies[pieces].start()
    w_copies[pieces + 1].start()
    for copy in cache_copies:
        copy.start()
    signal_all(place)
    for i in range(pieces):
        x_copies[i].wait()
        w_copies[i].wait()
        add_query(i, i == 0, hidden, wq_buf, q_acc)
    wait_all(place)
    outgoing = exchange_query(place, q_acc, q_send, q_out, q_ssem, q_rsem)
    chip_rows = residual.shape[1]
    for j in range(CHUNKS):
        residual[j] = hidden[place.core * CHUNKS + j, aligned(place.chip, chip_rows), :]
    w_copies[pieces].wait()
    w_copies[pieces + 1].wait()
    new_rows(place, hidden, wkv_buf, kv_new)
    for copy in query_copies(place, q_send, q_out, q_ssem, q_rsem, True):
        copy.wait_recv()
    for copy in outgoing:
        copy.wait_send()
    for copy in cache_copies:
        copy.wait()


def mix_kernel(count, last, layer, *refs):
    refs = list(refs)
    take = lambda k: [refs.pop(0) for _ in range(k)]
    context, residual, wo = take(3)
    if not last:
        wq, wk, wv, k_cache, v_cache = take(5)
        q_out, kv_new, next_residual, k_vmem, v_vmem = take(5)
    else:
        (hidden,) = take(1)
    c_recv, wo_far, wo_own, p_send, p_recv, total, s1_recv, comb, s2_left, s2_right = take(10)
    wo_sems, c_ssem, c_rsem, p_ssem, p_rsem, s1_ssem, s1_rsem = take(7)
    s2_ssem, s2_rsem, ag_ssem, ag_rsem, fw_ssem, fw_rsem, d2d_ssem, d2d_rsem = take(8)
    if not last:
        hidden, wq_buf, wkv_buf, q_acc, q_send, w_sems, cache_sems, q_ssem, q_rsem = take(9)
    place = Place(count)
    heads, rows, head_dim = c_recv.shape
    local_rows = rows // count
    chip_rows = rows // CHIPS
    depth = hidden.shape[-1]
    half = depth * CHUNKS

    wo_copies = []
    for j in range(CHUNKS):
        wo_copies.append(pltpu.make_async_copy(
            wo.at[layer, :, aligned((1 - place.core) * CHUNKS + j, depth)], wo_far.at[j], wo_sems.at[j]))
    for j in range(CHUNKS):
        wo_copies.append(pltpu.make_async_copy(
            wo.at[layer, :, aligned(place.core * CHUNKS + j, depth)], wo_own.at[j], wo_sems.at[CHUNKS + j]))
    for copy in wo_copies:
        copy.start()
    if not last:
        w_copies = weight_copies(layer + 1, wq, wk, wv, wq_buf, wkv_buf, w_sems)
        cache_copies = [
            pltpu.make_async_copy(k_cache.at[layer + 1], k_vmem, cache_sems.at[0]),
            pltpu.make_async_copy(v_cache.at[layer + 1], v_vmem, cache_sems.at[1]),
        ]
        for copy in w_copies + cache_copies:
            copy.start()

    signal_all(place)
    c_recv[:, aligned(place.me, local_rows), :] = context[pl.ds(place.me * heads, heads)]
    wait_all(place)

    def context_copy(offset, source):
        target = place.peer(offset)
        return remote(
            context.at[pl.ds(target * heads, heads)], c_recv.at[:, aligned(source, local_rows), :],
            c_ssem.at[offset], c_rsem.at[offset], target)

    sends = []

    def send(copy):
        copy.start()
        sends.append(copy)

    for offset in send_order(count):
        send(context_copy(offset, place.me))
    for offset in range(1, count):
        context_copy(offset, place.origin(offset)).wait_recv()

    def product(weights):
        acc = None
        for pair in range(heads // 2):
            lhs = jnp.concatenate([c_recv[2 * pair], c_recv[2 * pair + 1]], axis=1)
            part = jnp.dot(lhs, weights[pl.ds(pair * 2 * head_dim, 2 * head_dim), :], preferred_element_type=F32)
            acc = part if acc is None else acc + part
        return acc

    def pair_copy(j):
        return remote(p_send.at[j], p_recv.at[j], p_ssem.at[j], p_rsem.at[j], place.sibling)

    def block(chip):
        return aligned(chip, chip_rows)

    for j in range(CHUNKS):
        wo_copies[j].wait()
        p_send[j] = product(wo_far.at[j])
        send(pair_copy(j))

    def step_one(j):
        target = place.to_right if j % 2 == 0 else place.to_left
        return remote(total.at[j, block(place.across), :], s1_recv.at[j], s1_ssem.at[j], s1_rsem.at[j], target)

    def step_two(j, rightward, source):
        target = place.to_right if rightward else place.to_left
        inbox = s2_left if rightward else s2_right
        slot = j if rightward else CHUNKS + j
        return remote(source, inbox.at[j], s2_ssem.at[slot], s2_rsem.at[slot], target)

    for j in range(CHUNKS):
        wo_copies[CHUNKS + j].wait()
        own = product(wo_own.at[j])
        pair_copy(j).wait_recv()
        total[j] = own + p_recv[j]
        send(step_one(j))
        rightward = j % 2 == 1
        send(step_two(j, rightward, total.at[j, block(place.right if rightward else place.left), :]))
    for j in range(CHUNKS):
        step_one(j).wait_recv()
        rightward = j % 2 == 0
        comb[j] = total[j, block(place.right if rightward else place.left), :] + s1_recv[j]
        send(step_two(j, rightward, comb.at[j]))

    def piece(core, j):
        return core * CHUNKS + j

    def gather_copy(j, way, chip):
        target = place.to_right if way == 0 else place.to_left
        region = hidden.at[piece(place.core, j), block(chip), :]
        return remote(region, region, ag_ssem.at[way * CHUNKS + j], ag_rsem.at[way * CHUNKS + j], target)

    def forward_copy(j, chip):
        target = place.to_right if j % 2 == 0 else place.to_left
        region = hidden.at[piece(place.core, j), block(chip), :]
        return remote(region, region, fw_ssem.at[j], fw_rsem.at[j], target)

    def twin_copy(j, kind, core):
        chip = (place.chip, place.left, place.right, place.across)[kind]
        region = hidden.at[piece(core, j), block(chip), :]
        slot = kind * CHUNKS + j
        return remote(region, region, d2d_ssem.at[slot], d2d_rsem.at[slot], place.sibling)

    def finish(j):
        step_two(j, True, comb.at[j]).wait_recv()
        step_two(j, False, comb.at[j]).wait_recv()
        summed = total[j, block(place.chip), :] + s2_left[j] + s2_right[j]
        value = (residual[j].astype(F32) + summed).astype(BF16)
        hidden[piece(place.core, j), block(place.chip), :] = value
        if not last:
            next_residual[j] = value
        send(gather_copy(j, 0, place.chip))
        send(gather_copy(j, 1, place.chip))
        send(twin_copy(j, 0, place.core))

    def pass_on(j):
        gather_copy(j, 0, place.left).wait_recv()
        if j % 2 == 0:
            send(forward_copy(j, place.left))
        send(twin_copy(j, 1, place.core))
        gather_copy(j, 1, place.right).wait_recv()
        if j % 2 == 1:
            send(forward_copy(j, place.right))
        send(twin_copy(j, 2, place.core))

    def far_block(j):
        forward_copy(j, place.across).wait_recv()
        send(twin_copy(j, 3, place.core))

    for j in range(CHUNKS):
        finish(j)
        if j >= 1:
            pass_on(j - 1)
        if j >= 2:
            far_block(j - 2)
            if not last:
                w_copies[2 * (j - 2)].wait()
                w_copies[2 * (j - 2) + 1].wait()
    pass_on(CHUNKS - 1)
    if not last:
        for i in range(2 * (CHUNKS - 2), len(w_copies)):
            w_copies[i].wait()
        for j in range(CHUNKS - 2):
            add_query(piece(place.core, j), j == 0, hidden, wq_buf, q_acc)
    far_block(CHUNKS - 2)
    if not last:
        add_query(piece(place.core, CHUNKS - 2), False, hidden, wq_buf, q_acc)
    far_block(CHUNKS - 1)
    if not last:
        add_query(piece(place.core, CHUNKS - 1), False, hidden, wq_buf, q_acc)
    for j in range(CHUNKS):
        for kind in range(4):
            twin_copy(j, kind, 1 - place.core).wait_recv()
        if not last:
            add_query(piece(1 - place.core, j), False, hidden, wq_buf, q_acc)
    if not last:
        outgoing = exchange_query(place, q_acc, q_send, q_out, q_ssem, q_rsem)
        new_rows(place, hidden, wkv_buf, kv_new)
        for copy in query_copies(place, q_send, q_out, q_ssem, q_rsem, True):
            copy.wait_recv()
        sends.extend(outgoing)
        for copy in cache_copies:
            copy.wait()
    for copy in sends:
        copy.wait_send()


GROUP = 4


def attention_kernel(layer, *refs):
    lens, q, kv_new, k_in, v_in = refs[:5]
    refs = refs[5:]
    if layer > 0:
        refs = refs[2:]
    k_out, v_out, k_buf, v_buf, context, q_rows, c_rows, sems = refs
    del k_in, v_in
    heads, local_rows, head_dim = q.shape
    seq_len = k_buf.shape[1]
    tile = 16

    for b in range(local_rows):
        start = pl.multiple_of((lens[b] // tile) * tile, tile)
        here = lax.broadcasted_iota(jnp.int32, (tile, head_dim), 0) == lens[b] - start
        for buf, column in ((k_buf, 0), (v_buf, head_dim)):
            fresh = jnp.broadcast_to(kv_new[b:b + 1, column:column + head_dim], (tile, head_dim))
            old = buf[b, pl.ds(start, tile), :].astype(F32)
            buf[b, pl.ds(start, tile), :] = jnp.where(here, fresh, old).astype(BF16)
    q_rows[...] = q[...].astype(F32).reshape(heads * local_rows, head_dim)
    writes = [
        pltpu.make_async_copy(k_buf, k_out.at[layer], sems.at[0]),
        pltpu.make_async_copy(v_buf, v_out.at[layer], sems.at[1]),
    ]
    for copy in writes:
        copy.start()

    def attend(b, span):
        rows = pl.ds(b, heads, stride=local_rows)
        query = q_rows[rows, :].astype(BF16)
        scores = lax.dot_general(
            query, k_buf[b, pl.ds(0, span), :], (((1,), (1,)), ((), ())), preferred_element_type=F32)
        scores = scores * (head_dim ** -0.5)
        visible = lax.broadcasted_iota(jnp.int32, (heads, span), 1) <= lens[b]
        scores = jnp.where(visible, scores, -jnp.inf)
        top = jnp.max(scores, axis=1, keepdims=True)
        powers = jnp.exp(scores - top)
        weights = (powers / jnp.sum(powers, axis=1, keepdims=True)).astype(BF16)
        out = jnp.dot(weights, v_buf[b, pl.ds(0, span), :], preferred_element_type=F32)
        c_rows[rows, :] = out.astype(BF16).astype(F32)

    spans = []
    span = 256
    while span < seq_len:
        spans.append(span)
        span *= 2
    spans.append(seq_len)

    def one_group(g, _):
        longest = lens[g * GROUP]
        for i in range(1, GROUP):
            longest = jnp.maximum(longest, lens[g * GROUP + i])
        low = 0
        for span in spans:
            @pl.when(jnp.logical_and(longest >= low, longest < span))
            def _(span=span):
                for i in range(GROUP):
                    attend(g * GROUP + i, span)
            low = span
        return 0

    lax.fori_loop(0, local_rows // GROUP, one_group, 0)
    context[...] = c_rows[...].reshape(heads, local_rows, head_dim).astype(BF16)
    for copy in writes:
        copy.wait()


def store_kernel(hidden, out, sems):
    pieces, rows, depth = hidden.shape
    copies = [pltpu.make_async_copy(hidden.at[i], out.at[:, pl.ds(i * depth, depth)], sems.at[i]) for i in range(pieces)]
    for copy in copies:
        copy.start()
    for copy in copies:
        copy.wait()


def solution(mesh):
    count = mesh.shape["model"]
    assert count == 2 * CHIPS
    row_axes = ("replica", "model")
    cache_spec = P(None, row_axes, None, None)
    DMA = pltpu.SemaphoreType.DMA

    def device_step(x, cache_len, w_query, w_key, w_value, w_out, k_cache, v_cache):
        rows, width = x.shape
        layers, local_rows, seq_len, head_dim = k_cache.shape
        local_width = w_query.shape[-1]
        local_heads = local_width // head_dim
        heads = local_heads * count
        pieces = 2 * CHUNKS
        depth = width // pieces
        chip_rows = rows // CHIPS
        my_len = lax.dynamic_slice_in_dim(cache_len, lax.axis_index("model") * local_rows, local_rows)
        w_query, w_key, w_value, w_out = map(to_hbm, (w_query, w_key, w_value, w_out))
        x, k_cache, v_cache = map(to_hbm, (x, k_cache, v_cache))

        project_out = (
            pltpu.VMEM((heads, local_rows, head_dim), BF16),
            pltpu.VMEM((local_rows, 2 * head_dim), F32),
            pltpu.VMEM((CHUNKS, chip_rows, depth), BF16),
            pltpu.VMEM(k_cache.shape[1:], BF16),
            pltpu.VMEM(v_cache.shape[1:], BF16),
        )
        project_scratch = [
            pltpu.VMEM((pieces, rows, depth), BF16),
            pltpu.VMEM((width, local_width), BF16),
            pltpu.VMEM((width, 2 * head_dim), BF16),
            pltpu.VMEM((rows, local_width), F32),
            pltpu.VMEM((local_heads, rows, head_dim), BF16),
        ]
        project_sems = [DMA((pieces + 2,)), DMA((2,)), DMA((count,)), DMA((count,))]
        mix_scratch = [
            pltpu.VMEM((local_heads, rows, head_dim), BF16),
            pltpu.VMEM((CHUNKS, local_width, depth), BF16),
            pltpu.VMEM((CHUNKS, local_width, depth), BF16),
            pltpu.VMEM((CHUNKS, rows, depth), F32),
            pltpu.VMEM((CHUNKS, rows, depth), F32),
            pltpu.VMEM((CHUNKS, rows, depth), F32),
            pltpu.VMEM((CHUNKS, chip_rows, depth), F32),
            pltpu.VMEM((CHUNKS, chip_rows, depth), F32),
            pltpu.VMEM((CHUNKS, chip_rows, depth), F32),
            pltpu.VMEM((CHUNKS, chip_rows, depth), F32),
            DMA((pieces,)), DMA((count,)), DMA((count,)), DMA((CHUNKS,)), DMA((CHUNKS,)), DMA((CHUNKS,)), DMA((CHUNKS,)),
            DMA((2 * CHUNKS,)), DMA((2 * CHUNKS,)), DMA((2 * CHUNKS,)), DMA((2 * CHUNKS,)),
            DMA((CHUNKS,)), DMA((CHUNKS,)), DMA((4 * CHUNKS,)), DMA((4 * CHUNKS,)),
        ]

        def params(collective_id, limit):
            return pltpu.CompilerParams(collective_id=collective_id, has_side_effects=True, vmem_limit_bytes=limit * MIB)

        query, kv_new, residual, k_vmem, v_vmem = pl.pallas_call(
            functools.partial(first_kernel, count),
            out_shape=project_out,
            in_specs=[ANY_SPEC] * 6,
            out_specs=(VMEM_SPEC,) * 5,
            scratch_shapes=project_scratch + [DMA((pieces,))] + project_sems,
            compiler_params=params(0, 16),
            name="first",
        )(x, w_query, w_key, w_value, k_cache, v_cache)

        k_new_cache = v_new_cache = None
        for layer in range(layers):
            last = layer == layers - 1
            operands = [my_len, query, kv_new, k_vmem, v_vmem]
            specs = [SMEM_SPEC] + [VMEM_SPEC] * 4
            aliases = {3: 2, 4: 3}
            if layer > 0:
                operands += [k_new_cache, v_new_cache]
                specs += [ANY_SPEC] * 2
                aliases |= {5: 0, 6: 1}
            k_new_cache, v_new_cache, _, _, context = pl.pallas_call(
                functools.partial(attention_kernel, layer),
                out_shape=(
                    pltpu.HBM(k_cache.shape, BF16),
                    pltpu.HBM(v_cache.shape, BF16),
                    pltpu.VMEM(k_cache.shape[1:], BF16),
                    pltpu.VMEM(v_cache.shape[1:], BF16),
                    pltpu.VMEM((heads, local_rows, head_dim), BF16),
                ),
                in_specs=specs,
                out_specs=(ANY_SPEC, ANY_SPEC, VMEM_SPEC, VMEM_SPEC, VMEM_SPEC),
                input_output_aliases=aliases,
                scratch_shapes=[
                    pltpu.VMEM((heads * local_rows, head_dim), F32),
                    pltpu.VMEM((heads * local_rows, head_dim), F32),
                    DMA((2,)),
                ],
                compiler_params=pltpu.CompilerParams(vmem_limit_bytes=16 * MIB),
                name=f"attend{layer}",
            )(*operands)
            if not last:
                query, kv_new, residual, k_vmem, v_vmem = pl.pallas_call(
                    functools.partial(mix_kernel, count, False, layer),
                    out_shape=project_out,
                    in_specs=[VMEM_SPEC] * 2 + [ANY_SPEC] * 6,
                    out_specs=(VMEM_SPEC,) * 5,
                    scratch_shapes=mix_scratch + project_scratch + project_sems,
                    compiler_params=params(1 + layer, 28),
                    name=f"mix{layer}",
                )(context, residual, w_out, w_query, w_key, w_value, k_cache, v_cache)
            else:
                hidden = pl.pallas_call(
                    functools.partial(mix_kernel, count, True, layer),
                    out_shape=pltpu.VMEM((pieces, rows, depth), BF16),
                    in_specs=[VMEM_SPEC] * 2 + [ANY_SPEC],
                    out_specs=VMEM_SPEC,
                    scratch_shapes=mix_scratch,
                    compiler_params=params(1 + layer, 20),
                    name=f"mix{layer}",
                )(context, residual, w_out)
        out = pl.pallas_call(
            store_kernel,
            out_shape=jax.ShapeDtypeStruct((rows, width), BF16),
            in_specs=[VMEM_SPEC],
            out_specs=ANY_SPEC,
            scratch_shapes=[DMA((pieces,))],
            name="store",
        )(hidden)
        return out, k_new_cache, v_new_cache

    return jax.shard_map(
        device_step,
        mesh=mesh,
        in_specs=(P("replica", None), P("replica"), P(None, None, "model"), P(), P(), P(None, "model", None), cache_spec, cache_spec),
        out_specs=(P("replica", None), cache_spec, cache_spec),
        check_vma=False,
    )
```

time: 252 us -> 99.9 us (0.40); the launches traced: 249 us -> 99.7 us
  Pallas kernels: 0 us -> 97.3 us
  waiting for transfers between devices: 95 us -> 0 us
  matrix products: 61 us -> 0 us
  other arithmetic: 50.6 us -> 0 us
  starting transfers between devices: 16.2 us -> 0 us
  between operations: 14.2 us -> 0.68 us
  blocking collectives: 8.57 us -> 0 us
    pallas_call x0 -> x6, Pallas kernels: none -> 97.3 us  [the longest x1 36.8 us: device_step(): pl.pallas_call(functools.partial(mix_kernel, count, False, layer), out_sh...]
    psum x2 -> x0, waiting for transfers between devices: 89.8 us -> none  [device_step(): total = lax.psum(part_sum, 'model')]
    dot_general x10 -> x0, matrix products: 38.8 us -> none  [the longest x2 19.6 us: attend_rows(): jnp.einsum('bhs,bsd->bhd', weights, v_layer, preferred_element_type=jnp.f...]
    select_n x1 -> x0, other arithmetic: 22.8 us -> none  [write_token(): jnp.where(positions == cache_len[:, None, None], new_rows[:, None, :], ca...]
    another operation x1 -> x0, other arithmetic: 22.8 us -> none  [device_step(): return (hidden, jnp.stack(k_layers), jnp.stack(v_layers))]
    sub x2 -> x0, matrix products: 22.3 us -> none  [attend_rows(): weights = jax.nn.softmax(scores, axis=-1).astype(jnp.bfloat16)]
    all_to_all x3 -> x0, starting transfers between devices: 16.2 us -> none  [the longest x2 12 us: device_step(): query = lax.all_to_all(query, 'model', 0, 1, tiled=True)]
    all_to_all x1 -> x0, blocking collectives: 8.57 us -> none  [device_step(): context = lax.all_to_all(context, 'model', 1, 0, tiled=True)]
  transfers between devices with their start and end apart: 5 -> 0, of which waited for: 4 -> 0; matrix products, arithmetic and copies ran while one was open for 20% -> 0% of each run, Pallas kernels for 0% -> 0%
where the time goes in v1:
time: 99.9 us; the launch traced here: 99.7 us
  Pallas kernels  97.3 us (97%)
  local copies, waits for them, and re-layouts  1.69 us (2%)
    pallas_call x1, Pallas kernels, device_step(): pl.pallas_call(functools.partial(mix_kernel, count, False, layer), out_sh...  36.8 us
    pallas_call x1, Pallas kernels, device_step(): pl.pallas_call(functools.partial(mix_kernel, count, True, layer), out_sha...  31.8 us
    pallas_call x2, Pallas kernels, device_step(): pl.pallas_call(functools.partial(attention_kernel, layer), out_shape=(plt...  14.6 us
    pallas_call x1, Pallas kernels, device_step(): pl.pallas_call(functools.partial(first_kernel, count), out_shape=project_...  11.8 us
    pallas_call x1, Pallas kernels, device_step(): pl.pallas_call(store_kernel, out_shape=jax.ShapeDtypeStruct((rows, width)...  2.25 us

profile of v1, /device:TPU:113, one launch (start us, length us, event | category | flops | bytes accessed | tf_op | source)
XLA Modules:
  0.0 99.7 jit_solution(4727293314594121678)
XLA Ops:
  0.6 0.7 dynamic_slice.3.refs_0_
  1.4 11.8 %first.1 = (bf16[32,16,128]{2,1,0:T(8,128)(2,1)S(1)}, f32[16,256]{1,0:T(8,128)S(1)}, bf16[4,32,512]{2,1,0:T(8,128)(2,1)S(1)}, bf16[16,2048,128]{2,1,0:T(8,128)(2,1)S(1)}, bf16[16,2048,128]{2,1,0:T(8,128)(2,1)S(1)}) custom-call(bf16[128,4096]{1,0:T(8,128)(2,1)} %x.1, bf16[2,4096,512]{2,1,0:T(8,128)(2,1)} %refs_3_.1, bf16[2,4096,128]{2,1,0:T(8,128)(2,1)} %refs_4_.1, ...), custom_call_target="tpu_custom_call" | custom-call | tf_op jit(solution)/shard_map/first/pallas_call | solution.py:489
  13.2 7.3 %attend0.1 = (bf16[2,16,2048,128]{3,2,1,0:T(8,128)(2,1)}, bf16[2,16,2048,128]{3,2,1,0:T(8,128)(2,1)}, bf16[16,2048,128]{2,1,0:T(8,128)(2,1)S(1)}, bf16[16,2048,1...) custom-call(s32[16]{0:T(128)S(1)} %dynamic_slice.3.refs_0_, ...), custom_call_target="tpu_custom_call", output_to_operand_aliasing={{2}: (3, {}), {3}: (4, {})} | custom-call | tf_op jit(solution)/shard_map/attend0/pallas_call | solution.py:509
  20.5 36.8 %mix0.1 = (bf16[32,16,128]{2,1,0:T(8,128)(2,1)S(1)}, f32[16,256]{1,0:T(8,128)S(1)}, bf16[4,32,512]{2,1,0:T(8,128)(2,1)S(1)}, bf16[16,2048,128]{2,1,0:T(8,128)(2,1)S(1)}, bf16[16,2048,128]{2,1,0:T(8,128)(2,1)S(1)}) custom-call(bf16[32,16,128]{2,1,0:T(8,128)(2,1)S(1)} %get-tuple-element.23.refs_0_, bf16[4,32,512]{2,1,0:T(8,128)(2,1)S(1)} %get-tuple-element.24.refs_1_, ...), custom_call_target="tpu_custom_call" | custom-call | tf_op jit(solution)/shard_map/mix0/pallas_call | solution.py:530
  57.3 7.3 %attend1.1 = (bf16[2,16,2048,128]{3,2,1,0:T(8,128)(2,1)}, bf16[2,16,2048,128]{3,2,1,0:T(8,128)(2,1)}, bf16[16,2048,128]{2,1,0:T(8,128)(2,1)S(1)}, bf16[16,2048,1...) custom-call(s32[16]{0:T(128)S(1)} %dynamic_slice.3.refs_0_, ...), custom_call_target="tpu_custom_call", output_to_operand_aliasing={{2}: (3, {}), {3}: (4, {}), {0}: (5, {}), {1}: (6, {})} | custom-call | tf_op jit(solution)/shard_map/attend1/pallas_call | solution.py:509
  64.7 31.8 %mix1.1.hidden = bf16[8,128,512]{2,1,0:T(8,128)(2,1)S(1)} custom-call(bf16[32,16,128]{2,1,0:T(8,128)(2,1)S(1)} %get-tuple-element.31.refs_0_, bf16[4,32,512]{2,1,0:T(8,128)(2,1)S(1)} %get-tuple-element.32.refs_1_, bf16[2,512,4096]{2,1,0:T(8,128)(2,1)} %refs_2_.3), custom_call_target="tpu_custom_call" | custom-call | tf_op jit(solution)/shard_map/mix1/pallas_call | solution.py:540
  96.5 0.0 copy-start
  96.5 1.0 copy-done
  97.4 2.2 %store.1 = bf16[128,4096]{1,0:T(8,128)(2,1)} custom-call(bf16[8,128,512]{2,1,0:T(8,128)(2,1)} %copy-done), custom_call_target="tpu_custom_call" | custom-call | tf_op jit(solution)/shard_map/store/pallas_call | solution.py:549
Async XLA Ops:
  96.5 1.0 copy-start

commit v2 on v1

--- a/solution.py
+++ b/solution.py
@@ -12,6 +12,8 @@
 BF16 = jnp.bfloat16
 CHIPS = 4
 CHUNKS = 4
+PARTS = 8
+RING = 0
 MIB = 1 << 20
 
 ANY_SPEC = pl.BlockSpec(memory_space=pltpu.HBM)
@@ -59,7 +61,7 @@
 
 def signal_all(place):
     barrier = pltpu.get_barrier_semaphore()
-    for offset in range(1, place.count):
+    for offset in send_order(place.count):
         pl.semaphore_signal(barrier, inc=1, device_id={"model": place.peer(offset)}, device_id_type=MESH)
 
 
@@ -80,6 +82,17 @@
     return copies
 
 
+def cache_loads(layer, k_cache, v_cache, k_vmem, v_vmem, sems):
+    parts = sems.shape[0] // 2
+    step = k_vmem.shape[0] // parts
+    copies = []
+    for i in range(parts):
+        part = pl.ds(i * step, step)
+        copies.append(pltpu.make_async_copy(k_cache.at[layer, part], k_vmem.at[part], sems.at[2 * i]))
+        copies.append(pltpu.make_async_copy(v_cache.at[layer, part], v_vmem.at[part], sems.at[2 * i + 1]))
+    return copies
+
+
 def add_query(piece, first, hidden, wq_buf, q_acc):
     depth = hidden.shape[-1]
     part = jnp.dot(hidden[piece], wq_buf[aligned(piece, depth), :], preferred_element_type=F32)
@@ -136,18 +149,15 @@
         pltpu.make_async_copy(x.at[:, pl.ds(i * depth, depth)], hidden.at[i], x_sems.at[i]) for i in range(pieces)
     ]
     w_copies = weight_copies(0, wq, wk, wv, wq_buf, wkv_buf, w_sems)
-    cache_copies = [
-        pltpu.make_async_copy(k_cache.at[0], k_vmem, cache_sems.at[0]),
-        pltpu.make_async_copy(v_cache.at[0], v_vmem, cache_sems.at[1]),
-    ]
+    cache_copies = cache_loads(0, k_cache, v_cache, k_vmem, v_vmem, cache_sems)
     for i in range(pieces):
         x_copies[i].start()
         w_copies[i].start()
+    signal_all(place)
     w_copies[pieces].start()
     w_copies[pieces + 1].start()
     for copy in cache_copies:
         copy.start()
-    signal_all(place)
     for i in range(pieces):
         x_copies[i].wait()
         w_copies[i].wait()
@@ -179,16 +189,16 @@
         (hidden,) = take(1)
     c_recv, wo_far, wo_own, p_send, p_recv, total, s1_recv, comb, s2_left, s2_right = take(10)
     wo_sems, c_ssem, c_rsem, p_ssem, p_rsem, s1_ssem, s1_rsem = take(7)
-    s2_ssem, s2_rsem, ag_ssem, ag_rsem, fw_ssem, fw_rsem, d2d_ssem, d2d_rsem = take(8)
+    s2_ssem, s2_rsem, ag_ssem, ag_rsem, d2d_ssem, d2d_rsem = take(6)
     if not last:
         hidden, wq_buf, wkv_buf, q_acc, q_send, w_sems, cache_sems, q_ssem, q_rsem = take(9)
     place = Place(count)
     heads, rows, head_dim = c_recv.shape
     local_rows = rows // count
     chip_rows = rows // CHIPS
-    depth = hidden.shape[-1]
-    half = depth * CHUNKS
-
+    depth = total.shape[-1]
+
+    signal_all(place)
     wo_copies = []
     for j in range(CHUNKS):
         wo_copies.append(pltpu.make_async_copy(
@@ -200,14 +210,10 @@
         copy.start()
     if not last:
         w_copies = weight_copies(layer + 1, wq, wk, wv, wq_buf, wkv_buf, w_sems)
-        cache_copies = [
-            pltpu.make_async_copy(k_cache.at[layer + 1], k_vmem, cache_sems.at[0]),
-            pltpu.make_async_copy(v_cache.at[layer + 1], v_vmem, cache_sems.at[1]),
-        ]
+        cache_copies = cache_loads(layer + 1, k_cache, v_cache, k_vmem, v_vmem, cache_sems)
         for copy in w_copies + cache_copies:
             copy.start()
 
-    signal_all(place)
     c_recv[:, aligned(place.me, local_rows), :] = context[pl.ds(place.me * heads, heads)]
     wait_all(place)
 
@@ -257,86 +263,99 @@
         slot = j if rightward else CHUNKS + j
         return remote(source, inbox.at[j], s2_ssem.at[slot], s2_rsem.at[slot], target)
 
+    def direct(j):
+        rightward = j % 2 == 1
+        send(step_two(j, rightward, total.at[j, block(place.right if rightward else place.left), :]))
+
+    def combine(j):
+        step_one(j).wait_recv()
+        rightward = j % 2 == 0
+        comb[j] = total[j, block(place.right if rightward else place.left), :] + s1_recv[j]
+        send(step_two(j, rightward, comb.at[j]))
+
     for j in range(CHUNKS):
         wo_copies[CHUNKS + j].wait()
         own = product(wo_own.at[j])
         pair_copy(j).wait_recv()
         total[j] = own + p_recv[j]
         send(step_one(j))
-        rightward = j % 2 == 1
-        send(step_two(j, rightward, total.at[j, block(place.right if rightward else place.left), :]))
-    for j in range(CHUNKS):
-        step_one(j).wait_recv()
-        rightward = j % 2 == 0
-        comb[j] = total[j, block(place.right if rightward else place.left), :] + s1_recv[j]
-        send(step_two(j, rightward, comb.at[j]))
+        if j == 0:
+            direct(0)
+        elif j >= 2:
+            direct(j - 1)
+    combine(0)
+    combine(1)
+    direct(CHUNKS - 1)
+    for j in range(2, CHUNKS):
+        combine(j)
 
     def piece(core, j):
         return core * CHUNKS + j
 
+    def region(core, j, chip):
+        if last:
+            return hidden.at[block(chip), aligned(piece(core, j), depth)]
+        return hidden.at[piece(core, j), block(chip), :]
+
     def gather_copy(j, way, chip):
-        target = place.to_right if way == 0 else place.to_left
-        region = hidden.at[piece(place.core, j), block(chip), :]
-        return remote(region, region, ag_ssem.at[way * CHUNKS + j], ag_rsem.at[way * CHUNKS + j], target)
+        target = (place.to_right, place.to_left, place.across * 2 + place.core)[way]
+        part = region(place.core, j, chip)
+        slot = way * CHUNKS + j
+        return remote(part, part, ag_ssem.at[slot], ag_rsem.at[slot], target)
 
     def forward_copy(j, chip):
         target = place.to_right if j % 2 == 0 else place.to_left
-        region = hidden.at[piece(place.core, j), block(chip), :]
-        return remote(region, region, fw_ssem.at[j], fw_rsem.at[j], target)
+        part = region(place.core, j, chip)
+        return remote(part, part, ag_ssem.at[2 * CHUNKS + j], ag_rsem.at[2 * CHUNKS + j], target)
 
     def twin_copy(j, kind, core):
         chip = (place.chip, place.left, place.right, place.across)[kind]
-        region = hidden.at[piece(core, j), block(chip), :]
+        part = region(core, j, chip)
         slot = kind * CHUNKS + j
-        return remote(region, region, d2d_ssem.at[slot], d2d_rsem.at[slot], place.sibling)
+        return remote(part, part, d2d_ssem.at[slot], d2d_rsem.at[slot], place.sibling)
 
     def finish(j):
         step_two(j, True, comb.at[j]).wait_recv()
         step_two(j, False, comb.at[j]).wait_recv()
         summed = total[j, block(place.chip), :] + s2_left[j] + s2_right[j]
         value = (residual[j].astype(F32) + summed).astype(BF16)
-        hidden[piece(place.core, j), block(place.chip), :] = value
-        if not last:
+        if last:
+            hidden[block(place.chip), aligned(piece(place.core, j), depth)] = value
+        else:
+            hidden[piece(place.core, j), block(place.chip), :] = value
             next_residual[j] = value
+        if j >= RING:
+            send(gather_copy(j, 2, place.chip))
         send(gather_copy(j, 0, place.chip))
         send(gather_copy(j, 1, place.chip))
         send(twin_copy(j, 0, place.core))
 
     def pass_on(j):
         gather_copy(j, 0, place.left).wait_recv()
-        if j % 2 == 0:
+        if j < RING and j % 2 == 0:
             send(forward_copy(j, place.left))
         send(twin_copy(j, 1, place.core))
         gather_copy(j, 1, place.right).wait_recv()
-        if j % 2 == 1:
+        if j < RING and j % 2 == 1:
             send(forward_copy(j, place.right))
         send(twin_copy(j, 2, place.core))
 
     def far_block(j):
-        forward_copy(j, place.across).wait_recv()
+        gather_copy(j, 2, place.across).wait_recv()
         send(twin_copy(j, 3, place.core))
 
     for j in range(CHUNKS):
         finish(j)
-        if j >= 1:
-            pass_on(j - 1)
         if j >= 2:
-            far_block(j - 2)
-            if not last:
-                w_copies[2 * (j - 2)].wait()
-                w_copies[2 * (j - 2) + 1].wait()
-    pass_on(CHUNKS - 1)
-    if not last:
-        for i in range(2 * (CHUNKS - 2), len(w_copies)):
-            w_copies[i].wait()
-        for j in range(CHUNKS - 2):
+            pass_on(j - 2)
+    for j in range(CHUNKS):
+        if j >= 2:
+            pass_on(j)
+        far_block(j)
+        if not last:
+            for copy in w_copies if j == 0 else ():
+                copy.wait()
             add_query(piece(place.core, j), j == 0, hidden, wq_buf, q_acc)
-    far_block(CHUNKS - 2)
-    if not last:
-        add_query(piece(place.core, CHUNKS - 2), False, hidden, wq_buf, q_acc)
-    far_block(CHUNKS - 1)
-    if not last:
-        add_query(piece(place.core, CHUNKS - 1), False, hidden, wq_buf, q_acc)
     for j in range(CHUNKS):
         for kind in range(4):
             twin_copy(j, kind, 1 - place.core).wait_recv()
@@ -354,11 +373,12 @@
         copy.wait_send()
 
 
-GROUP = 4
+GROUP = 8
+SHORT = 256
 
 
 def attention_kernel(layer, *refs):
-    lens, q, kv_new, k_in, v_in = refs[:5]
+    all_lens, q, kv_new, k_in, v_in = refs[:5]
     refs = refs[5:]
     if layer > 0:
         refs = refs[2:]
@@ -367,68 +387,74 @@
     heads, local_rows, head_dim = q.shape
     seq_len = k_buf.shape[1]
     tile = 16
+    first_row = lax.axis_index("model") * local_rows
+
+    def length(b):
+        return all_lens[first_row + b]
 
     for b in range(local_rows):
-        start = pl.multiple_of((lens[b] // tile) * tile, tile)
-        here = lax.broadcasted_iota(jnp.int32, (tile, head_dim), 0) == lens[b] - start
+        start = pl.multiple_of((length(b) // tile) * tile, tile)
+        here = lax.broadcasted_iota(jnp.int32, (tile, head_dim), 0) == length(b) - start
         for buf, column in ((k_buf, 0), (v_buf, head_dim)):
             fresh = jnp.broadcast_to(kv_new[b:b + 1, column:column + head_dim], (tile, head_dim))
             old = buf[b, pl.ds(start, tile), :].astype(F32)
             buf[b, pl.ds(start, tile), :] = jnp.where(here, fresh, old).astype(BF16)
+
     q_rows[...] = q[...].astype(F32).reshape(heads * local_rows, head_dim)
-    writes = [
-        pltpu.make_async_copy(k_buf, k_out.at[layer], sems.at[0]),
-        pltpu.make_async_copy(v_buf, v_out.at[layer], sems.at[1]),
-    ]
+    writes = []
+    parts = sems.shape[0] // 2
+    step = local_rows // parts
+    for i in range(parts):
+        part = pl.ds(i * step, step)
+        writes.append(pltpu.make_async_copy(k_buf.at[part], k_out.at[layer, part], sems.at[2 * i]))
+        writes.append(pltpu.make_async_copy(v_buf.at[part], v_out.at[layer, part], sems.at[2 * i + 1]))
     for copy in writes:
         copy.start()
 
-    def attend(b, span):
-        rows = pl.ds(b, heads, stride=local_rows)
-        query = q_rows[rows, :].astype(BF16)
-        scores = lax.dot_general(
-            query, k_buf[b, pl.ds(0, span), :], (((1,), (1,)), ((), ())), preferred_element_type=F32)
-        scores = scores * (head_dim ** -0.5)
-        visible = lax.broadcasted_iota(jnp.int32, (heads, span), 1) <= lens[b]
-        scores = jnp.where(visible, scores, -jnp.inf)
-        top = jnp.max(scores, axis=1, keepdims=True)
-        powers = jnp.exp(scores - top)
-        weights = (powers / jnp.sum(powers, axis=1, keepdims=True)).astype(BF16)
-        out = jnp.dot(weights, v_buf[b, pl.ds(0, span), :], preferred_element_type=F32)
-        c_rows[rows, :] = out.astype(BF16).astype(F32)
+    def attend(members, span):
+        rows = [pl.ds(b, heads, stride=local_rows) for b in members]
+        scores = [
+            lax.dot_general(
+                q_rows[r, :].astype(BF16), k_buf[b, pl.ds(0, span), :], (((1,), (1,)), ((), ())),
+                preferred_element_type=F32)
+            for b, r in zip(members, rows)
+        ]
+        positions = lax.broadcasted_iota(jnp.int32, (heads, span), 1)
+        scores = [jnp.where(positions <= length(b), s * (head_dim ** -0.5), -jnp.inf) for b, s in zip(members, scores)]
+        tops = [jnp.max(s, axis=1, keepdims=True) for s in scores]
+        powers = [jnp.exp(s - t) for s, t in zip(scores, tops)]
+        sums = [jnp.sum(p, axis=1, keepdims=True) for p in powers]
+        weights = [(p / t).astype(BF16) for p, t in zip(powers, sums)]
+        outs = [
+            jnp.dot(w, v_buf[b, pl.ds(0, span), :], preferred_element_type=F32) for b, w in zip(members, weights)
+        ]
+        for r, out in zip(rows, outs):
+            c_rows[r, :] = out.astype(BF16).astype(F32)
+
+    for first in range(0, local_rows, GROUP):
+        attend(list(range(first, first + GROUP)), SHORT)
 
     spans = []
-    span = 256
+    span = 2 * SHORT
     while span < seq_len:
         spans.append(span)
         span *= 2
     spans.append(seq_len)
 
-    def one_group(g, _):
-        longest = lens[g * GROUP]
-        for i in range(1, GROUP):
-            longest = jnp.maximum(longest, lens[g * GROUP + i])
-        low = 0
-        for span in spans:
-            @pl.when(jnp.logical_and(longest >= low, longest < span))
-            def _(span=span):
-                for i in range(GROUP):
-                    attend(g * GROUP + i, span)
-            low = span
+    def longer(b, _):
+        @pl.when(length(b) >= SHORT)
+        def _():
+            low = SHORT
+            for span in spans:
+                @pl.when(jnp.logical_and(length(b) >= low, length(b) < span))
+                def _(span=span):
+                    attend([b], span)
+                low = span
         return 0
 
-    lax.fori_loop(0, local_rows // GROUP, one_group, 0)
+    lax.fori_loop(0, local_rows, longer, 0)
     context[...] = c_rows[...].reshape(heads, local_rows, head_dim).astype(BF16)
     for copy in writes:
-        copy.wait()
-
-
-def store_kernel(hidden, out, sems):
-    pieces, rows, depth = hidden.shape
-    copies = [pltpu.make_async_copy(hidden.at[i], out.at[:, pl.ds(i * depth, depth)], sems.at[i]) for i in range(pieces)]
-    for copy in copies:
-        copy.start()
-    for copy in copies:
         copy.wait()
 
 
@@ -448,7 +474,6 @@
         pieces = 2 * CHUNKS
         depth = width // pieces
         chip_rows = rows // CHIPS
-        my_len = lax.dynamic_slice_in_dim(cache_len, lax.axis_index("model") * local_rows, local_rows)
         w_query, w_key, w_value, w_out = map(to_hbm, (w_query, w_key, w_value, w_out))
         x, k_cache, v_cache = map(to_hbm, (x, k_cache, v_cache))
 
@@ -466,7 +491,7 @@
             pltpu.VMEM((rows, local_width), F32),
             pltpu.VMEM((local_heads, rows, head_dim), BF16),
         ]
-        project_sems = [DMA((pieces + 2,)), DMA((2,)), DMA((count,)), DMA((count,))]
+        project_sems = [DMA((pieces + 2,)), DMA((2 * PARTS,)), DMA((count,)), DMA((count,))]
         mix_scratch = [
             pltpu.VMEM((local_heads, rows, head_dim), BF16),
             pltpu.VMEM((CHUNKS, local_width, depth), BF16),
@@ -479,8 +504,8 @@
             pltpu.VMEM((CHUNKS, chip_rows, depth), F32),
             pltpu.VMEM((CHUNKS, chip_rows, depth), F32),
             DMA((pieces,)), DMA((count,)), DMA((count,)), DMA((CHUNKS,)), DMA((CHUNKS,)), DMA((CHUNKS,)), DMA((CHUNKS,)),
-            DMA((2 * CHUNKS,)), DMA((2 * CHUNKS,)), DMA((2 * CHUNKS,)), DMA((2 * CHUNKS,)),
-            DMA((CHUNKS,)), DMA((CHUNKS,)), DMA((4 * CHUNKS,)), DMA((4 * CHUNKS,)),
+            DMA((2 * CHUNKS,)), DMA((2 * CHUNKS,)), DMA((3 * CHUNKS,)), DMA((3 * CHUNKS,)),
+            DMA((4 * CHUNKS,)), DMA((4 * CHUNKS,)),
         ]
 
         def params(collective_id, limit):
@@ -499,7 +524,7 @@
         k_new_cache = v_new_cache = None
         for layer in range(layers):
             last = layer == layers - 1
-            operands = [my_len, query, kv_new, k_vmem, v_vmem]
+            operands = [cache_len, query, kv_new, k_vmem, v_vmem]
             specs = [SMEM_SPEC] + [VMEM_SPEC] * 4
             aliases = {3: 2, 4: 3}
             if layer > 0:
@@ -521,7 +546,7 @@
                 scratch_shapes=[
                     pltpu.VMEM((heads * local_rows, head_dim), F32),
                     pltpu.VMEM((heads * local_rows, head_dim), F32),
-                    DMA((2,)),
+                    DMA((2 * PARTS,)),
                 ],
                 compiler_params=pltpu.CompilerParams(vmem_limit_bytes=16 * MIB),
                 name=f"attend{layer}",
@@ -539,22 +564,14 @@
             else:
                 hidden = pl.pallas_call(
                     functools.partial(mix_kernel, count, True, layer),
-                    out_shape=pltpu.VMEM((pieces, rows, depth), BF16),
+                    out_shape=pltpu.VMEM((rows, width), BF16),
                     in_specs=[VMEM_SPEC] * 2 + [ANY_SPEC],
                     out_specs=VMEM_SPEC,
                     scratch_shapes=mix_scratch,
                     compiler_params=params(1 + layer, 20),
                     name=f"mix{layer}",
                 )(context, residual, w_out)
-        out = pl.pallas_call(
-            store_kernel,
-            out_shape=jax.ShapeDtypeStruct((rows, width), BF16),
-            in_specs=[VMEM_SPEC],
-            out_specs=ANY_SPEC,
-            scratch_shapes=[DMA((pieces,))],
-            name="store",
-        )(hidden)
-        return out, k_new_cache, v_new_cache
+        return hidden, k_new_cache, v_new_cache
 
     return jax.shard_map(
         device_step,

time: 99.9 us -> 85.3 us (0.85)
  Pallas kernels: 97.3 us -> 83.5 us
    pallas_call x1, Pallas kernels: 31.8 us -> 26.6 us  [device_step(): pl.pallas_call(functools.partial(mix_kernel, count, True, layer), out_sha...]
    pallas_call x1, Pallas kernels: 36.8 us -> 33.7 us  [device_step(): pl.pallas_call(functools.partial(mix_kernel, count, False, layer), out_sh...]
    pallas_call x1, Pallas kernels: 11.8 us -> 9.36 us  [device_step(): pl.pallas_call(functools.partial(first_kernel, count), out_shape=project_...]
    pallas_call x1 -> x0, Pallas kernels: 2.25 us -> none  [device_step(): pl.pallas_call(store_kernel, out_shape=jax.ShapeDtypeStruct((rows, width)...]
where the time goes in v2:
time: 85.3 us; the launch traced here: 85.2 us
  Pallas kernels  83.5 us (98%)
  local copies, waits for them, and re-layouts  0.98 us (1%)
    pallas_call x1, Pallas kernels, device_step(): pl.pallas_call(functools.partial(mix_kernel, count, False, layer), out_sh...  33.7 us
    pallas_call x1, Pallas kernels, device_step(): pl.pallas_call(functools.partial(mix_kernel, count, True, layer), out_sha...  26.6 us
    pallas_call x2, Pallas kernels, device_step(): pl.pallas_call(functools.partial(attention_kernel, layer), out_shape=(plt...  13.9 us
    pallas_call x1, Pallas kernels, device_step(): pl.pallas_call(functools.partial(first_kernel, count), out_shape=project_...  9.36 us

profile of v2, /device:TPU:113, one launch (start us, length us, event | category | flops | bytes accessed | tf_op | source)
XLA Modules:
  0.0 85.2 jit_solution(6611001759666434913)
XLA Ops:
  0.6 0.0 copy-start
  0.6 9.4 %first.1 = (bf16[32,16,128]{2,1,0:T(8,128)(2,1)S(1)}, f32[16,256]{1,0:T(8,128)S(1)}, bf16[4,32,512]{2,1,0:T(8,128)(2,1)S(1)}, bf16[16,2048,128]{2,1,0:T(8,128)(2,1)S(1)}, bf16[16,2048,128]{2,1,0:T(8,128)(2,1)S(1)}) custom-call(bf16[128,4096]{1,0:T(8,128)(2,1)} %x.1, bf16[2,4096,512]{2,1,0:T(8,128)(2,1)} %refs_3_.1, bf16[2,4096,128]{2,1,0:T(8,128)(2,1)} %refs_4_.1, ...), custom_call_target="tpu_custom_call" | custom-call | tf_op jit(solution)/shard_map/first/pallas_call | solution.py:514
  10.0 0.0 copy-done
  10.0 6.9 %attend0.1 = (bf16[2,16,2048,128]{3,2,1,0:T(8,128)(2,1)}, bf16[2,16,2048,128]{3,2,1,0:T(8,128)(2,1)}, bf16[16,2048,128]{2,1,0:T(8,128)(2,1)S(1)}, bf16[16,2048,1...) custom-call(s32[128]{0:T(128)S(1)} %copy-done, ...), custom_call_target="tpu_custom_call", output_to_operand_aliasing={{2}: (3, {}), {3}: (4, {})} | custom-call | tf_op jit(solution)/shard_map/attend0/pallas_call | solution.py:534
  17.0 33.7 %mix0.1 = (bf16[32,16,128]{2,1,0:T(8,128)(2,1)S(1)}, f32[16,256]{1,0:T(8,128)S(1)}, bf16[4,32,512]{2,1,0:T(8,128)(2,1)S(1)}, bf16[16,2048,128]{2,1,0:T(8,128)(2,1)S(1)}, bf16[16,2048,128]{2,1,0:T(8,128)(2,1)S(1)}) custom-call(bf16[32,16,128]{2,1,0:T(8,128)(2,1)S(1)} %get-tuple-element.23.refs_0_, bf16[4,32,512]{2,1,0:T(8,128)(2,1)S(1)} %get-tuple-element.24.refs_1_, ...), custom_call_target="tpu_custom_call" | custom-call | tf_op jit(solution)/shard_map/mix0/pallas_call | solution.py:555
  50.6 6.9 %attend1.1 = (bf16[2,16,2048,128]{3,2,1,0:T(8,128)(2,1)}, bf16[2,16,2048,128]{3,2,1,0:T(8,128)(2,1)}, bf16[16,2048,128]{2,1,0:T(8,128)(2,1)S(1)}, bf16[16,2048,1...) custom-call(s32[128]{0:T(128)S(1)} %copy-done, ...), custom_call_target="tpu_custom_call", output_to_operand_aliasing={{2}: (3, {}), {3}: (4, {}), {0}: (5, {}), {1}: (6, {})} | custom-call | tf_op jit(solution)/shard_map/attend1/pallas_call | solution.py:534
  57.6 26.6 %mix1.1 = bf16[128,4096]{1,0:T(8,128)(2,1)S(1)} custom-call(bf16[32,16,128]{2,1,0:T(8,128)(2,1)S(1)} %get-tuple-element.31.refs_0_, bf16[4,32,512]{2,1,0:T(8,128)(2,1)S(1)} %get-tuple-element.32.refs_1_, bf16[2,512,4096]{2,1,0:T(8,128)(2,1)} %refs_2_.3), custom_call_target="tpu_custom_call" | custom-call | tf_op jit(solution)/shard_map/mix1/pallas_call | solution.py:565
  84.2 1.0 %copy.24 = bf16[128,4096]{1,0:T(8,128)(2,1)} copy(bf16[128,4096]{1,0:T(8,128)(2,1)S(1)} %mix1.1) | data formatting | bytes 2097152
Async XLA Ops:
  0.6 9.4 %copy-start = (s32[128]{0:T(128)S(1)}, s32[128]{0:T(128)}, u32[]{:S(2)}) copy-start(s32[128]{0:T(128)} %refs_0_.3) | copy-start | bytes 1540

commit v3 on v2

--- a/solution.py
+++ b/solution.py
@@ -13,7 +13,7 @@
 CHIPS = 4
 CHUNKS = 4
 PARTS = 8
-RING = 0
+RING = 3
 MIB = 1 << 20
 
 ANY_SPEC = pl.BlockSpec(memory_space=pltpu.HBM)
@@ -275,9 +275,10 @@
 
     for j in range(CHUNKS):
         wo_copies[CHUNKS + j].wait()
-        own = product(wo_own.at[j])
+        total[j] = product(wo_own.at[j])
+    for j in range(CHUNKS):
         pair_copy(j).wait_recv()
-        total[j] = own + p_recv[j]
+        total[j] += p_recv[j]
         send(step_one(j))
         if j == 0:
             direct(0)
@@ -346,10 +347,10 @@
 
     for j in range(CHUNKS):
         finish(j)
-        if j >= 2:
-            pass_on(j - 2)
-    for j in range(CHUNKS):
-        if j >= 2:
+    for j in range(RING):
+        pass_on(j)
+    for j in range(CHUNKS):
+        if j >= RING:
             pass_on(j)
         far_block(j)
         if not last:
@@ -392,24 +393,26 @@
     def length(b):
         return all_lens[first_row + b]
 
-    for b in range(local_rows):
-        start = pl.multiple_of((length(b) // tile) * tile, tile)
-        here = lax.broadcasted_iota(jnp.int32, (tile, head_dim), 0) == length(b) - start
-        for buf, column in ((k_buf, 0), (v_buf, head_dim)):
-            fresh = jnp.broadcast_to(kv_new[b:b + 1, column:column + head_dim], (tile, head_dim))
-            old = buf[b, pl.ds(start, tile), :].astype(F32)
-            buf[b, pl.ds(start, tile), :] = jnp.where(here, fresh, old).astype(BF16)
-
-    q_rows[...] = q[...].astype(F32).reshape(heads * local_rows, head_dim)
     writes = []
     parts = sems.shape[0] // 2
     step = local_rows // parts
     for i in range(parts):
+        for b in range(i * step, (i + 1) * step):
+            start = pl.multiple_of((length(b) // tile) * tile, tile)
+            here = lax.broadcasted_iota(jnp.int32, (tile, head_dim), 0) == length(b) - start
+            for buf, column in ((k_buf, 0), (v_buf, head_dim)):
+                fresh = jnp.broadcast_to(kv_new[b:b + 1, column:column + head_dim], (tile, head_dim))
+                old = buf[b, pl.ds(start, tile), :].astype(F32)
+                buf[b, pl.ds(start, tile), :] = jnp.where(here, fresh, old).astype(BF16)
         part = pl.ds(i * step, step)
         writes.append(pltpu.make_async_copy(k_buf.at[part], k_out.at[layer, part], sems.at[2 * i]))
         writes.append(pltpu.make_async_copy(v_buf.at[part], v_out.at[layer, part], sems.at[2 * i + 1]))
-    for copy in writes:
-        copy.start()
+        if i > 0:
+            writes[2 * i - 2].start()
+            writes[2 * i - 1].start()
+    q_rows[...] = q[...].astype(F32).reshape(heads * local_rows, head_dim)
+    writes[-2].start()
+    writes[-1].start()
 
     def attend(members, span):
         rows = [pl.ds(b, heads, stride=local_rows) for b in members]

time: 85.3 us -> 86.4 us (1.013)
  Pallas kernels: 83.5 us -> 84.6 us
    pallas_call x1, Pallas kernels: 33.7 us -> 35.3 us  [device_step(): pl.pallas_call(functools.partial(mix_kernel, count, False, layer), out_sh...]
where the time goes in v3:
time: 86.4 us; the launch traced here: 86.3 us
  Pallas kernels  84.6 us (98%)
  local copies, waits for them, and re-layouts  0.98 us (1%)
    pallas_call x1, Pallas kernels, device_step(): pl.pallas_call(functools.partial(mix_kernel, count, False, layer), out_sh...  35.3 us
    pallas_call x1, Pallas kernels, device_step(): pl.pallas_call(functools.partial(mix_kernel, count, True, layer), out_sha...  26.9 us
    pallas_call x2, Pallas kernels, device_step(): pl.pallas_call(functools.partial(attention_kernel, layer), out_shape=(plt...  13.1 us
    pallas_call x1, Pallas kernels, device_step(): pl.pallas_call(functools.partial(first_kernel, count), out_shape=project_...  9.36 us

profile of v3, /device:TPU:113, one launch (start us, length us, event | category | flops | bytes accessed | tf_op | source)
XLA Modules:
  0.0 86.3 jit_solution(7214961838620132416)
XLA Ops:
  0.6 0.0 copy-start
  0.6 9.4 %first.1 = (bf16[32,16,128]{2,1,0:T(8,128)(2,1)S(1)}, f32[16,256]{1,0:T(8,128)S(1)}, bf16[4,32,512]{2,1,0:T(8,128)(2,1)S(1)}, bf16[16,2048,128]{2,1,0:T(8,128)(2,1)S(1)}, bf16[16,2048,128]{2,1,0:T(8,128)(2,1)S(1)}) custom-call(bf16[128,4096]{1,0:T(8,128)(2,1)} %x.1, bf16[2,4096,512]{2,1,0:T(8,128)(2,1)} %refs_3_.1, bf16[2,4096,128]{2,1,0:T(8,128)(2,1)} %refs_4_.1, ...), custom_call_target="tpu_custom_call" | custom-call | tf_op jit(solution)/shard_map/first/pallas_call | solution.py:517
  10.0 0.0 copy-done
  10.0 6.5 %attend0.1 = (bf16[2,16,2048,128]{3,2,1,0:T(8,128)(2,1)}, bf16[2,16,2048,128]{3,2,1,0:T(8,128)(2,1)}, bf16[16,2048,128]{2,1,0:T(8,128)(2,1)S(1)}, bf16[16,2048,1...) custom-call(s32[128]{0:T(128)S(1)} %copy-done, ...), custom_call_target="tpu_custom_call", output_to_operand_aliasing={{2}: (3, {}), {3}: (4, {})} | custom-call | tf_op jit(solution)/shard_map/attend0/pallas_call | solution.py:537
  16.6 35.3 %mix0.1 = (bf16[32,16,128]{2,1,0:T(8,128)(2,1)S(1)}, f32[16,256]{1,0:T(8,128)S(1)}, bf16[4,32,512]{2,1,0:T(8,128)(2,1)S(1)}, bf16[16,2048,128]{2,1,0:T(8,128)(2,1)S(1)}, bf16[16,2048,128]{2,1,0:T(8,128)(2,1)S(1)}) custom-call(bf16[32,16,128]{2,1,0:T(8,128)(2,1)S(1)} %get-tuple-element.23.refs_0_, bf16[4,32,512]{2,1,0:T(8,128)(2,1)S(1)} %get-tuple-element.24.refs_1_, ...), custom_call_target="tpu_custom_call" | custom-call | tf_op jit(solution)/shard_map/mix0/pallas_call | solution.py:558
  51.9 6.5 %attend1.1 = (bf16[2,16,2048,128]{3,2,1,0:T(8,128)(2,1)}, bf16[2,16,2048,128]{3,2,1,0:T(8,128)(2,1)}, bf16[16,2048,128]{2,1,0:T(8,128)(2,1)S(1)}, bf16[16,2048,1...) custom-call(s32[128]{0:T(128)S(1)} %copy-done, ...), custom_call_target="tpu_custom_call", output_to_operand_aliasing={{2}: (3, {}), {3}: (4, {}), {0}: (5, {}), {1}: (6, {})} | custom-call | tf_op jit(solution)/shard_map/attend1/pallas_call | solution.py:537
  58.4 26.9 %mix1.1 = bf16[128,4096]{1,0:T(8,128)(2,1)S(1)} custom-call(bf16[32,16,128]{2,1,0:T(8,128)(2,1)S(1)} %get-tuple-element.31.refs_0_, bf16[4,32,512]{2,1,0:T(8,128)(2,1)S(1)} %get-tuple-element.32.refs_1_, bf16[2,512,4096]{2,1,0:T(8,128)(2,1)} %refs_2_.3), custom_call_target="tpu_custom_call" | custom-call | tf_op jit(solution)/shard_map/mix1/pallas_call | solution.py:568
  85.3 1.0 %copy.24 = bf16[128,4096]{1,0:T(8,128)(2,1)} copy(bf16[128,4096]{1,0:T(8,128)(2,1)S(1)} %mix1.1) | data formatting | bytes 2097152
Async XLA Ops:
  0.6 9.4 %copy-start = (s32[128]{0:T(128)S(1)}, s32[128]{0:T(128)}, u32[]{:S(2)}) copy-start(s32[128]{0:T(128)} %refs_0_.3) | copy-start | bytes 1540

commit v4 on v3

--- a/solution.py
+++ b/solution.py
@@ -13,7 +13,8 @@
 CHIPS = 4
 CHUNKS = 4
 PARTS = 8
-RING = 3
+RING = 0
+RELAYED = 4
 MIB = 1 << 20
 
 ANY_SPEC = pl.BlockSpec(memory_space=pltpu.HBM)
@@ -255,6 +256,8 @@
 
     def step_one(j):
         target = place.to_right if j % 2 == 0 else place.to_left
+        if j >= RELAYED:
+            target = place.across * 2 + place.core
         return remote(total.at[j, block(place.across), :], s1_recv.at[j], s1_ssem.at[j], s1_rsem.at[j], target)
 
     def step_two(j, rightward, source):
@@ -264,8 +267,8 @@
         return remote(source, inbox.at[j], s2_ssem.at[slot], s2_rsem.at[slot], target)
 
     def direct(j):
-        rightward = j % 2 == 1
-        send(step_two(j, rightward, total.at[j, block(place.right if rightward else place.left), :]))
+        for rightward in (j % 2 == 1, j % 2 == 0) if j >= RELAYED else (j % 2 == 1,):
+            send(step_two(j, rightward, total.at[j, block(place.right if rightward else place.left), :]))
 
     def combine(j):
         step_one(j).wait_recv()
@@ -280,14 +283,15 @@
         pair_copy(j).wait_recv()
         total[j] += p_recv[j]
         send(step_one(j))
-        if j == 0:
-            direct(0)
+        if j == 0 or j >= RELAYED:
+            direct(j)
         elif j >= 2:
             direct(j - 1)
-    combine(0)
-    combine(1)
-    direct(CHUNKS - 1)
-    for j in range(2, CHUNKS):
+    for j in range(min(RELAYED, 2)):
+        combine(j)
+    if RELAYED == CHUNKS:
+        direct(CHUNKS - 1)
+    for j in range(2, RELAYED):
         combine(j)
 
     def piece(core, j):
@@ -319,6 +323,9 @@
         step_two(j, True, comb.at[j]).wait_recv()
         step_two(j, False, comb.at[j]).wait_recv()
         summed = total[j, block(place.chip), :] + s2_left[j] + s2_right[j]
+        if j >= RELAYED:
+            step_one(j).wait_recv()
+            summed = summed + s1_recv[j]
         value = (residual[j].astype(F32) + summed).astype(BF16)
         if last:
             hidden[block(place.chip), aligned(piece(place.core, j), depth)] = value

time: 86.4 us -> 84.9 us (0.983)
  Pallas kernels: 84.6 us -> 83.2 us
    pallas_call x1, Pallas kernels: 35.3 us -> 34.2 us  [device_step(): pl.pallas_call(functools.partial(mix_kernel, count, False, layer), out_sh...]
where the time goes in v4:
time: 84.9 us
  Pallas kernels  83.2 us (98%)
  local copies, waits for them, and re-layouts  0.98 us (1%)
    pallas_call x1, Pallas kernels, device_step(): pl.pallas_call(functools.partial(mix_kernel, count, False, layer), out_sh...  34.2 us
    pallas_call x1, Pallas kernels, device_step(): pl.pallas_call(functools.partial(mix_kernel, count, True, layer), out_sha...  26.5 us
    pallas_call x2, Pallas kernels, device_step(): pl.pallas_call(functools.partial(attention_kernel, layer), out_shape=(plt...  13.1 us
    pallas_call x1, Pallas kernels, device_step(): pl.pallas_call(functools.partial(first_kernel, count), out_shape=project_...  9.36 us

profile of v4, /device:TPU:113, one launch (start us, length us, event | category | flops | bytes accessed | tf_op | source)
XLA Modules:
  0.0 84.9 jit_solution(4409003939295011861)
XLA Ops:
  0.6 0.0 copy-start
  0.6 9.4 %first.1 = (bf16[32,16,128]{2,1,0:T(8,128)(2,1)S(1)}, f32[16,256]{1,0:T(8,128)S(1)}, bf16[4,32,512]{2,1,0:T(8,128)(2,1)S(1)}, bf16[16,2048,128]{2,1,0:T(8,128)(2,1)S(1)}, bf16[16,2048,128]{2,1,0:T(8,128)(2,1)S(1)}) custom-call(bf16[128,4096]{1,0:T(8,128)(2,1)} %x.1, bf16[2,4096,512]{2,1,0:T(8,128)(2,1)} %refs_3_.1, bf16[2,4096,128]{2,1,0:T(8,128)(2,1)} %refs_4_.1, ...), custom_call_target="tpu_custom_call" | custom-call | tf_op jit(solution)/shard_map/first/pallas_call | solution.py:524
  10.0 0.0 copy-done
  10.0 6.5 %attend0.1 = (bf16[2,16,2048,128]{3,2,1,0:T(8,128)(2,1)}, bf16[2,16,2048,128]{3,2,1,0:T(8,128)(2,1)}, bf16[16,2048,128]{2,1,0:T(8,128)(2,1)S(1)}, bf16[16,2048,1...) custom-call(s32[128]{0:T(128)S(1)} %copy-done, ...), custom_call_target="tpu_custom_call", output_to_operand_aliasing={{2}: (3, {}), {3}: (4, {})} | custom-call | tf_op jit(solution)/shard_map/attend0/pallas_call | solution.py:544
  16.6 34.2 %mix0.1 = (bf16[32,16,128]{2,1,0:T(8,128)(2,1)S(1)}, f32[16,256]{1,0:T(8,128)S(1)}, bf16[4,32,512]{2,1,0:T(8,128)(2,1)S(1)}, bf16[16,2048,128]{2,1,0:T(8,128)(2,1)S(1)}, bf16[16,2048,128]{2,1,0:T(8,128)(2,1)S(1)}) custom-call(bf16[32,16,128]{2,1,0:T(8,128)(2,1)S(1)} %get-tuple-element.23.refs_0_, bf16[4,32,512]{2,1,0:T(8,128)(2,1)S(1)} %get-tuple-element.24.refs_1_, ...), custom_call_target="tpu_custom_call" | custom-call | tf_op jit(solution)/shard_map/mix0/pallas_call | solution.py:565
  50.8 6.5 %attend1.1 = (bf16[2,16,2048,128]{3,2,1,0:T(8,128)(2,1)}, bf16[2,16,2048,128]{3,2,1,0:T(8,128)(2,1)}, bf16[16,2048,128]{2,1,0:T(8,128)(2,1)S(1)}, bf16[16,2048,1...) custom-call(s32[128]{0:T(128)S(1)} %copy-done, ...), custom_call_target="tpu_custom_call", output_to_operand_aliasing={{2}: (3, {}), {3}: (4, {}), {0}: (5, {}), {1}: (6, {})} | custom-call | tf_op jit(solution)/shard_map/attend1/pallas_call | solution.py:544
  57.4 26.5 %mix1.1 = bf16[128,4096]{1,0:T(8,128)(2,1)S(1)} custom-call(bf16[32,16,128]{2,1,0:T(8,128)(2,1)S(1)} %get-tuple-element.31.refs_0_, bf16[4,32,512]{2,1,0:T(8,128)(2,1)S(1)} %get-tuple-element.32.refs_1_, bf16[2,512,4096]{2,1,0:T(8,128)(2,1)} %refs_2_.3), custom_call_target="tpu_custom_call" | custom-call | tf_op jit(solution)/shard_map/mix1/pallas_call | solution.py:575
  83.9 1.0 %copy.24 = bf16[128,4096]{1,0:T(8,128)(2,1)} copy(bf16[128,4096]{1,0:T(8,128)(2,1)S(1)} %mix1.1) | data formatting | bytes 2097152
Async XLA Ops:
  0.6 9.4 %copy-start = (s32[128]{0:T(128)S(1)}, s32[128]{0:T(128)}, u32[]{:S(2)}) copy-start(s32[128]{0:T(128)} %refs_0_.3) | copy-start | bytes 1540

commit v5 on v4

--- a/solution.py
+++ b/solution.py
@@ -11,10 +11,10 @@
 F32 = jnp.float32
 BF16 = jnp.bfloat16
 CHIPS = 4
-CHUNKS = 4
+CHUNKS = 8
 PARTS = 8
 RING = 0
-RELAYED = 4
+RELAYED = CHUNKS
 MIB = 1 << 20
 
 ANY_SPEC = pl.BlockSpec(memory_space=pltpu.HBM)
@@ -279,18 +279,21 @@
     for j in range(CHUNKS):
         wo_copies[CHUNKS + j].wait()
         total[j] = product(wo_own.at[j])
+    pending = []
     for j in range(CHUNKS):
         pair_copy(j).wait_recv()
         total[j] += p_recv[j]
         send(step_one(j))
-        if j == 0 or j >= RELAYED:
+        while pending:
+            direct(pending.pop())
+        if 0 < j < RELAYED:
+            pending.append(j)
+        else:
             direct(j)
-        elif j >= 2:
-            direct(j - 1)
     for j in range(min(RELAYED, 2)):
         combine(j)
-    if RELAYED == CHUNKS:
-        direct(CHUNKS - 1)
+    while pending:
+        direct(pending.pop())
     for j in range(2, RELAYED):
         combine(j)
 

time: 84.9 us -> 89.1 us (1.049)
  Pallas kernels: 83.2 us -> 87.3 us
    pallas_call x1, Pallas kernels: 26.5 us -> 29.1 us  [device_step(): pl.pallas_call(functools.partial(mix_kernel, count, True, layer), out_sha...]
    pallas_call x1, Pallas kernels: 34.2 us -> 35.6 us  [device_step(): pl.pallas_call(functools.partial(mix_kernel, count, False, layer), out_sh...]
where the time goes in v5:
time: 89.1 us; the launch traced here: 89 us
  Pallas kernels  87.3 us (98%)
  local copies, waits for them, and re-layouts  0.98 us (1%)
    pallas_call x1, Pallas kernels, device_step(): pl.pallas_call(functools.partial(mix_kernel, count, False, layer), out_sh...  35.6 us
    pallas_call x1, Pallas kernels, device_step(): pl.pallas_call(functools.partial(mix_kernel, count, True, layer), out_sha...  29.1 us
    pallas_call x2, Pallas kernels, device_step(): pl.pallas_call(functools.partial(attention_kernel, layer), out_shape=(plt...  13.1 us
    pallas_call x1, Pallas kernels, device_step(): pl.pallas_call(functools.partial(first_kernel, count), out_shape=project_...  9.44 us

profile of v5, /device:TPU:113, one launch (start us, length us, event | category | flops | bytes accessed | tf_op | source)
XLA Modules:
  0.0 89.0 jit_solution(6638351493167028283)
XLA Ops:
  0.6 0.0 copy-start
  0.6 9.4 %first.1 = (bf16[32,16,128]{2,1,0:T(8,128)(2,1)S(1)}, f32[16,256]{1,0:T(8,128)S(1)}, bf16[8,32,256]{2,1,0:T(8,128)(2,1)S(1)}, bf16[16,2048,128]{2,1,0:T(8,128)(2,1)S(1)}, bf16[16,2048,128]{2,1,0:T(8,128)(2,1)S(1)}) custom-call(bf16[128,4096]{1,0:T(8,128)(2,1)} %x.1, bf16[2,4096,512]{2,1,0:T(8,128)(2,1)} %refs_3_.1, bf16[2,4096,128]{2,1,0:T(8,128)(2,1)} %refs_4_.1, ...), custom_call_target="tpu_custom_call" | custom-call | tf_op jit(solution)/shard_map/first/pallas_call | solution.py:527
  10.1 0.0 copy-done
  10.1 6.5 %attend0.1 = (bf16[2,16,2048,128]{3,2,1,0:T(8,128)(2,1)}, bf16[2,16,2048,128]{3,2,1,0:T(8,128)(2,1)}, bf16[16,2048,128]{2,1,0:T(8,128)(2,1)S(1)}, bf16[16,2048,1...) custom-call(s32[128]{0:T(128)S(1)} %copy-done, ...), custom_call_target="tpu_custom_call", output_to_operand_aliasing={{2}: (3, {}), {3}: (4, {})} | custom-call | tf_op jit(solution)/shard_map/attend0/pallas_call | solution.py:547
  16.7 35.6 %mix0.1 = (bf16[32,16,128]{2,1,0:T(8,128)(2,1)S(1)}, f32[16,256]{1,0:T(8,128)S(1)}, bf16[8,32,256]{2,1,0:T(8,128)(2,1)S(1)}, bf16[16,2048,128]{2,1,0:T(8,128)(2,1)S(1)}, bf16[16,2048,128]{2,1,0:T(8,128)(2,1)S(1)}) custom-call(bf16[32,16,128]{2,1,0:T(8,128)(2,1)S(1)} %get-tuple-element.23.refs_0_, bf16[8,32,256]{2,1,0:T(8,128)(2,1)S(1)} %get-tuple-element.24.refs_1_, ...), custom_call_target="tpu_custom_call" | custom-call | tf_op jit(solution)/shard_map/mix0/pallas_call | solution.py:568
  52.3 6.5 %attend1.1 = (bf16[2,16,2048,128]{3,2,1,0:T(8,128)(2,1)}, bf16[2,16,2048,128]{3,2,1,0:T(8,128)(2,1)}, bf16[16,2048,128]{2,1,0:T(8,128)(2,1)S(1)}, bf16[16,2048,1...) custom-call(s32[128]{0:T(128)S(1)} %copy-done, ...), custom_call_target="tpu_custom_call", output_to_operand_aliasing={{2}: (3, {}), {3}: (4, {}), {0}: (5, {}), {1}: (6, {})} | custom-call | tf_op jit(solution)/shard_map/attend1/pallas_call | solution.py:547
  58.9 29.1 %mix1.1 = bf16[128,4096]{1,0:T(8,128)(2,1)S(1)} custom-call(bf16[32,16,128]{2,1,0:T(8,128)(2,1)S(1)} %get-tuple-element.31.refs_0_, bf16[8,32,256]{2,1,0:T(8,128)(2,1)S(1)} %get-tuple-element.32.refs_1_, bf16[2,512,4096]{2,1,0:T(8,128)(2,1)} %refs_2_.3), custom_call_target="tpu_custom_call" | custom-call | tf_op jit(solution)/shard_map/mix1/pallas_call | solution.py:578
  88.0 1.0 %copy.24 = bf16[128,4096]{1,0:T(8,128)(2,1)} copy(bf16[128,4096]{1,0:T(8,128)(2,1)S(1)} %mix1.1) | data formatting | bytes 2097152
Async XLA Ops:
  0.6 9.5 %copy-start = (s32[128]{0:T(128)S(1)}, s32[128]{0:T(128)}, u32[]{:S(2)}) copy-start(s32[128]{0:T(128)} %refs_0_.3) | copy-start | bytes 1540

commit v6 on v5

--- a/solution.py
+++ b/solution.py
@@ -11,10 +11,10 @@
 F32 = jnp.float32
 BF16 = jnp.bfloat16
 CHIPS = 4
-CHUNKS = 8
+CHUNKS = 4
 PARTS = 8
 RING = 0
-RELAYED = CHUNKS
+RELAYED = 4
 MIB = 1 << 20
 
 ANY_SPEC = pl.BlockSpec(memory_space=pltpu.HBM)
@@ -316,11 +316,9 @@
         part = region(place.core, j, chip)
         return remote(part, part, ag_ssem.at[2 * CHUNKS + j], ag_rsem.at[2 * CHUNKS + j], target)
 
-    def twin_copy(j, kind, core):
-        chip = (place.chip, place.left, place.right, place.across)[kind]
-        part = region(core, j, chip)
-        slot = kind * CHUNKS + j
-        return remote(part, part, d2d_ssem.at[slot], d2d_rsem.at[slot], place.sibling)
+    def twin_copy(j, core):
+        part = hidden.at[:, aligned(piece(core, j), depth)] if last else hidden.at[piece(core, j)]
+        return remote(part, part, d2d_ssem.at[j], d2d_rsem.at[j], place.sibling)
 
     def finish(j):
         step_two(j, True, comb.at[j]).wait_recv()
@@ -339,21 +337,18 @@
             send(gather_copy(j, 2, place.chip))
         send(gather_copy(j, 0, place.chip))
         send(gather_copy(j, 1, place.chip))
-        send(twin_copy(j, 0, place.core))
 
     def pass_on(j):
         gather_copy(j, 0, place.left).wait_recv()
         if j < RING and j % 2 == 0:
             send(forward_copy(j, place.left))
-        send(twin_copy(j, 1, place.core))
         gather_copy(j, 1, place.right).wait_recv()
         if j < RING and j % 2 == 1:
             send(forward_copy(j, place.right))
-        send(twin_copy(j, 2, place.core))
 
     def far_block(j):
         gather_copy(j, 2, place.across).wait_recv()
-        send(twin_copy(j, 3, place.core))
+        send(twin_copy(j, place.core))
 
     for j in range(CHUNKS):
         finish(j)
@@ -368,8 +363,7 @@
                 copy.wait()
             add_query(piece(place.core, j), j == 0, hidden, wq_buf, q_acc)
     for j in range(CHUNKS):
-        for kind in range(4):
-            twin_copy(j, kind, 1 - place.core).wait_recv()
+        twin_copy(j, 1 - place.core).wait_recv()
         if not last:
             add_query(piece(1 - place.core, j), False, hidden, wq_buf, q_acc)
     if not last:
@@ -518,7 +512,7 @@
             pltpu.VMEM((CHUNKS, chip_rows, depth), F32),
             DMA((pieces,)), DMA((count,)), DMA((count,)), DMA((CHUNKS,)), DMA((CHUNKS,)), DMA((CHUNKS,)), DMA((CHUNKS,)),
             DMA((2 * CHUNKS,)), DMA((2 * CHUNKS,)), DMA((3 * CHUNKS,)), DMA((3 * CHUNKS,)),
-            DMA((4 * CHUNKS,)), DMA((4 * CHUNKS,)),
+            DMA((CHUNKS,)), DMA((CHUNKS,)),
         ]
 
         def params(collective_id, limit):

time: 89.1 us -> 84.6 us (0.949)
  Pallas kernels: 87.3 us -> 82.8 us
    pallas_call x1, Pallas kernels: 29.1 us -> 26.3 us  [device_step(): pl.pallas_call(functools.partial(mix_kernel, count, True, layer), out_sha...]
    pallas_call x1, Pallas kernels: 35.6 us -> 34.1 us  [device_step(): pl.pallas_call(functools.partial(mix_kernel, count, False, layer), out_sh...]
where the time goes in v6:
time: 84.6 us; the launch traced here: 84.5 us
  Pallas kernels  82.8 us (98%)
  local copies, waits for them, and re-layouts  0.98 us (1%)
    pallas_call x1, Pallas kernels, device_step(): pl.pallas_call(functools.partial(mix_kernel, count, False, layer), out_sh...  34.1 us
    pallas_call x1, Pallas kernels, device_step(): pl.pallas_call(functools.partial(mix_kernel, count, True, layer), out_sha...  26.3 us
    pallas_call x2, Pallas kernels, device_step(): pl.pallas_call(functools.partial(attention_kernel, layer), out_shape=(plt...  13.1 us
    pallas_call x1, Pallas kernels, device_step(): pl.pallas_call(functools.partial(first_kernel, count), out_shape=project_...  9.36 us

profile of v6, /device:TPU:113, one launch (start us, length us, event | category | flops | bytes accessed | tf_op | source)
XLA Modules:
  0.0 84.5 jit_solution(16186675710622417477)
XLA Ops:
  0.6 0.0 copy-start
  0.6 9.4 %first.1 = (bf16[32,16,128]{2,1,0:T(8,128)(2,1)S(1)}, f32[16,256]{1,0:T(8,128)S(1)}, bf16[4,32,512]{2,1,0:T(8,128)(2,1)S(1)}, bf16[16,2048,128]{2,1,0:T(8,128)(2,1)S(1)}, bf16[16,2048,128]{2,1,0:T(8,128)(2,1)S(1)}) custom-call(bf16[128,4096]{1,0:T(8,128)(2,1)} %x.1, bf16[2,4096,512]{2,1,0:T(8,128)(2,1)} %refs_3_.1, bf16[2,4096,128]{2,1,0:T(8,128)(2,1)} %refs_4_.1, ...), custom_call_target="tpu_custom_call" | custom-call | tf_op jit(solution)/shard_map/first/pallas_call | solution.py:521
  10.0 0.0 copy-done
  10.0 6.5 %attend0.1 = (bf16[2,16,2048,128]{3,2,1,0:T(8,128)(2,1)}, bf16[2,16,2048,128]{3,2,1,0:T(8,128)(2,1)}, bf16[16,2048,128]{2,1,0:T(8,128)(2,1)S(1)}, bf16[16,2048,1...) custom-call(s32[128]{0:T(128)S(1)} %copy-done, ...), custom_call_target="tpu_custom_call", output_to_operand_aliasing={{2}: (3, {}), {3}: (4, {})} | custom-call | tf_op jit(solution)/shard_map/attend0/pallas_call | solution.py:541
  16.6 34.1 %mix0.1 = (bf16[32,16,128]{2,1,0:T(8,128)(2,1)S(1)}, f32[16,256]{1,0:T(8,128)S(1)}, bf16[4,32,512]{2,1,0:T(8,128)(2,1)S(1)}, bf16[16,2048,128]{2,1,0:T(8,128)(2,1)S(1)}, bf16[16,2048,128]{2,1,0:T(8,128)(2,1)S(1)}) custom-call(bf16[32,16,128]{2,1,0:T(8,128)(2,1)S(1)} %get-tuple-element.23.refs_0_, bf16[4,32,512]{2,1,0:T(8,128)(2,1)S(1)} %get-tuple-element.24.refs_1_, ...), custom_call_target="tpu_custom_call" | custom-call | tf_op jit(solution)/shard_map/mix0/pallas_call | solution.py:562
  50.7 6.5 %attend1.1 = (bf16[2,16,2048,128]{3,2,1,0:T(8,128)(2,1)}, bf16[2,16,2048,128]{3,2,1,0:T(8,128)(2,1)}, bf16[16,2048,128]{2,1,0:T(8,128)(2,1)S(1)}, bf16[16,2048,1...) custom-call(s32[128]{0:T(128)S(1)} %copy-done, ...), custom_call_target="tpu_custom_call", output_to_operand_aliasing={{2}: (3, {}), {3}: (4, {}), {0}: (5, {}), {1}: (6, {})} | custom-call | tf_op jit(solution)/shard_map/attend1/pallas_call | solution.py:541
  57.3 26.3 %mix1.1 = bf16[128,4096]{1,0:T(8,128)(2,1)S(1)} custom-call(bf16[32,16,128]{2,1,0:T(8,128)(2,1)S(1)} %get-tuple-element.31.refs_0_, bf16[4,32,512]{2,1,0:T(8,128)(2,1)S(1)} %get-tuple-element.32.refs_1_, bf16[2,512,4096]{2,1,0:T(8,128)(2,1)} %refs_2_.3), custom_call_target="tpu_custom_call" | custom-call | tf_op jit(solution)/shard_map/mix1/pallas_call | solution.py:572
  83.5 1.0 %copy.24 = bf16[128,4096]{1,0:T(8,128)(2,1)} copy(bf16[128,4096]{1,0:T(8,128)(2,1)S(1)} %mix1.1) | data formatting | bytes 2097152
Async XLA Ops:
  0.6 9.4 %copy-start = (s32[128]{0:T(128)S(1)}, s32[128]{0:T(128)}, u32[]{:S(2)}) copy-start(s32[128]{0:T(128)} %refs_0_.3) | copy-start | bytes 1540

commit v7 on v6

--- a/solution.py
+++ b/solution.py
@@ -13,7 +13,7 @@
 CHIPS = 4
 CHUNKS = 4
 PARTS = 8
-RING = 0
+RING = 2
 RELAYED = 4
 MIB = 1 << 20
 
@@ -354,15 +354,16 @@
         finish(j)
     for j in range(RING):
         pass_on(j)
-    for j in range(CHUNKS):
+    order = list(range(RING, CHUNKS)) + list(range(RING))
+    for j in order:
         if j >= RING:
             pass_on(j)
         far_block(j)
         if not last:
-            for copy in w_copies if j == 0 else ():
+            for copy in w_copies if j == order[0] else ():
                 copy.wait()
-            add_query(piece(place.core, j), j == 0, hidden, wq_buf, q_acc)
-    for j in range(CHUNKS):
+            add_query(piece(place.core, j), j == order[0], hidden, wq_buf, q_acc)
+    for j in order:
         twin_copy(j, 1 - place.core).wait_recv()
         if not last:
             add_query(piece(1 - place.core, j), False, hidden, wq_buf, q_acc)

time: 84.6 us -> 84.5 us (level)
  no operation moved by 1% of the time
where the time goes in v7:
time: 84.5 us; the launch traced here: 84.4 us
  Pallas kernels  82.8 us (98%)
  local copies, waits for them, and re-layouts  0.98 us (1%)
    pallas_call x1, Pallas kernels, device_step(): pl.pallas_call(functools.partial(mix_kernel, count, False, layer), out_sh...  34.2 us
    pallas_call x1, Pallas kernels, device_step(): pl.pallas_call(functools.partial(mix_kernel, count, True, layer), out_sha...  26.1 us
    pallas_call x2, Pallas kernels, device_step(): pl.pallas_call(functools.partial(attention_kernel, layer), out_shape=(plt...  13.1 us
    pallas_call x1, Pallas kernels, device_step(): pl.pallas_call(functools.partial(first_kernel, count), out_shape=project_...  9.36 us

profile of v7, /device:TPU:113, one launch (start us, length us, event | category | flops | bytes accessed | tf_op | source)
XLA Modules:
  0.0 84.4 jit_solution(463126233950198287)
XLA Ops:
  0.6 0.0 copy-start
  0.6 9.4 %first.1 = (bf16[32,16,128]{2,1,0:T(8,128)(2,1)S(1)}, f32[16,256]{1,0:T(8,128)S(1)}, bf16[4,32,512]{2,1,0:T(8,128)(2,1)S(1)}, bf16[16,2048,128]{2,1,0:T(8,128)(2,1)S(1)}, bf16[16,2048,128]{2,1,0:T(8,128)(2,1)S(1)}) custom-call(bf16[128,4096]{1,0:T(8,128)(2,1)} %x.1, bf16[2,4096,512]{2,1,0:T(8,128)(2,1)} %refs_3_.1, bf16[2,4096,128]{2,1,0:T(8,128)(2,1)} %refs_4_.1, ...), custom_call_target="tpu_custom_call" | custom-call | tf_op jit(solution)/shard_map/first/pallas_call | solution.py:522
  10.0 0.0 copy-done
  10.0 6.5 %attend0.1 = (bf16[2,16,2048,128]{3,2,1,0:T(8,128)(2,1)}, bf16[2,16,2048,128]{3,2,1,0:T(8,128)(2,1)}, bf16[16,2048,128]{2,1,0:T(8,128)(2,1)S(1)}, bf16[16,2048,1...) custom-call(s32[128]{0:T(128)S(1)} %copy-done, ...), custom_call_target="tpu_custom_call", output_to_operand_aliasing={{2}: (3, {}), {3}: (4, {})} | custom-call | tf_op jit(solution)/shard_map/attend0/pallas_call | solution.py:542
  16.6 34.2 %mix0.1 = (bf16[32,16,128]{2,1,0:T(8,128)(2,1)S(1)}, f32[16,256]{1,0:T(8,128)S(1)}, bf16[4,32,512]{2,1,0:T(8,128)(2,1)S(1)}, bf16[16,2048,128]{2,1,0:T(8,128)(2,1)S(1)}, bf16[16,2048,128]{2,1,0:T(8,128)(2,1)S(1)}) custom-call(bf16[32,16,128]{2,1,0:T(8,128)(2,1)S(1)} %get-tuple-element.23.refs_0_, bf16[4,32,512]{2,1,0:T(8,128)(2,1)S(1)} %get-tuple-element.24.refs_1_, ...), custom_call_target="tpu_custom_call" | custom-call | tf_op jit(solution)/shard_map/mix0/pallas_call | solution.py:563
  50.8 6.5 %attend1.1 = (bf16[2,16,2048,128]{3,2,1,0:T(8,128)(2,1)}, bf16[2,16,2048,128]{3,2,1,0:T(8,128)(2,1)}, bf16[16,2048,128]{2,1,0:T(8,128)(2,1)S(1)}, bf16[16,2048,1...) custom-call(s32[128]{0:T(128)S(1)} %copy-done, ...), custom_call_target="tpu_custom_call", output_to_operand_aliasing={{2}: (3, {}), {3}: (4, {}), {0}: (5, {}), {1}: (6, {})} | custom-call | tf_op jit(solution)/shard_map/attend1/pallas_call | solution.py:542
  57.4 26.1 %mix1.1 = bf16[128,4096]{1,0:T(8,128)(2,1)S(1)} custom-call(bf16[32,16,128]{2,1,0:T(8,128)(2,1)S(1)} %get-tuple-element.31.refs_0_, bf16[4,32,512]{2,1,0:T(8,128)(2,1)S(1)} %get-tuple-element.32.refs_1_, bf16[2,512,4096]{2,1,0:T(8,128)(2,1)} %refs_2_.3), custom_call_target="tpu_custom_call" | custom-call | tf_op jit(solution)/shard_map/mix1/pallas_call | solution.py:573
  83.5 1.0 %copy.24 = bf16[128,4096]{1,0:T(8,128)(2,1)} copy(bf16[128,4096]{1,0:T(8,128)(2,1)S(1)} %mix1.1) | data formatting | bytes 2097152
Async XLA Ops:
  0.6 9.4 %copy-start = (s32[128]{0:T(128)S(1)}, s32[128]{0:T(128)}, u32[]{:S(2)}) copy-start(s32[128]{0:T(128)} %refs_0_.3) | copy-start | bytes 1540

commit v8 on v7

--- a/solution.py
+++ b/solution.py
@@ -43,8 +43,9 @@
         self.right = (self.chip + 1) % CHIPS
         self.left = (self.chip + CHIPS - 1) % CHIPS
         self.across = (self.chip + 2) % CHIPS
-        self.to_right = self.right * 2 + self.core
-        self.to_left = self.left * 2 + self.core
+        self.half = (self.core + self.chip) % 2
+        self.to_right = self.right * 2 + 1 - self.core
+        self.to_left = self.left * 2 + 1 - self.core
         self.sibling = self.chip * 2 + (1 - self.core)
 
     def peer(self, offset):
@@ -167,7 +168,7 @@
     outgoing = exchange_query(place, q_acc, q_send, q_out, q_ssem, q_rsem)
     chip_rows = residual.shape[1]
     for j in range(CHUNKS):
-        residual[j] = hidden[place.core * CHUNKS + j, aligned(place.chip, chip_rows), :]
+        residual[j] = hidden[place.half * CHUNKS + j, aligned(place.chip, chip_rows), :]
     w_copies[pieces].wait()
     w_copies[pieces + 1].wait()
     new_rows(place, hidden, wkv_buf, kv_new)
@@ -203,10 +204,10 @@
     wo_copies = []
     for j in range(CHUNKS):
         wo_copies.append(pltpu.make_async_copy(
-            wo.at[layer, :, aligned((1 - place.core) * CHUNKS + j, depth)], wo_far.at[j], wo_sems.at[j]))
+            wo.at[layer, :, aligned((1 - place.half) * CHUNKS + j, depth)], wo_far.at[j], wo_sems.at[j]))
     for j in range(CHUNKS):
         wo_copies.append(pltpu.make_async_copy(
-            wo.at[layer, :, aligned(place.core * CHUNKS + j, depth)], wo_own.at[j], wo_sems.at[CHUNKS + j]))
+            wo.at[layer, :, aligned(place.half * CHUNKS + j, depth)], wo_own.at[j], wo_sems.at[CHUNKS + j]))
     for copy in wo_copies:
         copy.start()
     if not last:
@@ -297,27 +298,27 @@
     for j in range(2, RELAYED):
         combine(j)
 
-    def piece(core, j):
-        return core * CHUNKS + j
-
-    def region(core, j, chip):
+    def piece(half, j):
+        return half * CHUNKS + j
+
+    def region(half, j, chip):
         if last:
-            return hidden.at[block(chip), aligned(piece(core, j), depth)]
-        return hidden.at[piece(core, j), block(chip), :]
+            return hidden.at[block(chip), aligned(piece(half, j), depth)]
+        return hidden.at[piece(half, j), block(chip), :]
 
     def gather_copy(j, way, chip):
         target = (place.to_right, place.to_left, place.across * 2 + place.core)[way]
-        part = region(place.core, j, chip)
+        part = region(place.half, j, chip)
         slot = way * CHUNKS + j
         return remote(part, part, ag_ssem.at[slot], ag_rsem.at[slot], target)
 
     def forward_copy(j, chip):
         target = place.to_right if j % 2 == 0 else place.to_left
-        part = region(place.core, j, chip)
+        part = region(place.half, j, chip)
         return remote(part, part, ag_ssem.at[2 * CHUNKS + j], ag_rsem.at[2 * CHUNKS + j], target)
 
-    def twin_copy(j, core):
-        part = hidden.at[:, aligned(piece(core, j), depth)] if last else hidden.at[piece(core, j)]
+    def twin_copy(j, half):
+        part = hidden.at[:, aligned(piece(half, j), depth)] if last else hidden.at[piece(half, j)]
         return remote(part, part, d2d_ssem.at[j], d2d_rsem.at[j], place.sibling)
 
     def finish(j):
@@ -329,9 +330,9 @@
             summed = summed + s1_recv[j]
         value = (residual[j].astype(F32) + summed).astype(BF16)
         if last:
-            hidden[block(place.chip), aligned(piece(place.core, j), depth)] = value
+            hidden[block(place.chip), aligned(piece(place.half, j), depth)] = value
         else:
-            hidden[piece(place.core, j), block(place.chip), :] = value
+            hidden[piece(place.half, j), block(place.chip), :] = value
             next_residual[j] = value
         if j >= RING:
             send(gather_copy(j, 2, place.chip))
@@ -348,7 +349,7 @@
 
     def far_block(j):
         gather_copy(j, 2, place.across).wait_recv()
-        send(twin_copy(j, place.core))
+        send(twin_copy(j, place.half))
 
     for j in range(CHUNKS):
         finish(j)
@@ -362,11 +363,11 @@
         if not last:
             for copy in w_copies if j == order[0] else ():
                 copy.wait()
-            add_query(piece(place.core, j), j == order[0], hidden, wq_buf, q_acc)
+            add_query(piece(place.half, j), j == order[0], hidden, wq_buf, q_acc)
     for j in order:
-        twin_copy(j, 1 - place.core).wait_recv()
+        twin_copy(j, 1 - place.half).wait_recv()
         if not last:
-            add_query(piece(1 - place.core, j), False, hidden, wq_buf, q_acc)
+            add_query(piece(1 - place.half, j), False, hidden, wq_buf, q_acc)
     if not last:
         outgoing = exchange_query(place, q_acc, q_send, q_out, q_ssem, q_rsem)
         new_rows(place, hidden, wkv_buf, kv_new)

time: 84.5 us -> 84.1 us (level)
  no operation moved by 1% of the time
where the time goes in v8:
time: 84.1 us; the launch traced here: 84 us
  Pallas kernels  82.3 us (98%)
  local copies, waits for them, and re-layouts  0.98 us (1%)
    pallas_call x1, Pallas kernels, device_step(): pl.pallas_call(functools.partial(mix_kernel, count, False, layer), out_sh...  33.8 us
    pallas_call x1, Pallas kernels, device_step(): pl.pallas_call(functools.partial(mix_kernel, count, True, layer), out_sha...  26.1 us
    pallas_call x2, Pallas kernels, device_step(): pl.pallas_call(functools.partial(attention_kernel, layer), out_shape=(plt...  13.1 us
    pallas_call x1, Pallas kernels, device_step(): pl.pallas_call(functools.partial(first_kernel, count), out_shape=project_...  9.36 us

profile of v8, /device:TPU:113, one launch (start us, length us, event | category | flops | bytes accessed | tf_op | source)
XLA Modules:
  0.0 84.0 jit_solution(13883772958883825092)
XLA Ops:
  0.6 0.0 copy-start
  0.6 9.4 %first.1 = (bf16[32,16,128]{2,1,0:T(8,128)(2,1)S(1)}, f32[16,256]{1,0:T(8,128)S(1)}, bf16[4,32,512]{2,1,0:T(8,128)(2,1)S(1)}, bf16[16,2048,128]{2,1,0:T(8,128)(2,1)S(1)}, bf16[16,2048,128]{2,1,0:T(8,128)(2,1)S(1)}) custom-call(bf16[128,4096]{1,0:T(8,128)(2,1)} %x.1, bf16[2,4096,512]{2,1,0:T(8,128)(2,1)} %refs_3_.1, bf16[2,4096,128]{2,1,0:T(8,128)(2,1)} %refs_4_.1, ...), custom_call_target="tpu_custom_call" | custom-call | tf_op jit(solution)/shard_map/first/pallas_call | solution.py:523
  10.0 0.0 copy-done
  10.0 6.5 %attend0.1 = (bf16[2,16,2048,128]{3,2,1,0:T(8,128)(2,1)}, bf16[2,16,2048,128]{3,2,1,0:T(8,128)(2,1)}, bf16[16,2048,128]{2,1,0:T(8,128)(2,1)S(1)}, bf16[16,2048,1...) custom-call(s32[128]{0:T(128)S(1)} %copy-done, ...), custom_call_target="tpu_custom_call", output_to_operand_aliasing={{2}: (3, {}), {3}: (4, {})} | custom-call | tf_op jit(solution)/shard_map/attend0/pallas_call | solution.py:543
  16.6 33.8 %mix0.1 = (bf16[32,16,128]{2,1,0:T(8,128)(2,1)S(1)}, f32[16,256]{1,0:T(8,128)S(1)}, bf16[4,32,512]{2,1,0:T(8,128)(2,1)S(1)}, bf16[16,2048,128]{2,1,0:T(8,128)(2,1)S(1)}, bf16[16,2048,128]{2,1,0:T(8,128)(2,1)S(1)}) custom-call(bf16[32,16,128]{2,1,0:T(8,128)(2,1)S(1)} %get-tuple-element.23.refs_0_, bf16[4,32,512]{2,1,0:T(8,128)(2,1)S(1)} %get-tuple-element.24.refs_1_, ...), custom_call_target="tpu_custom_call" | custom-call | tf_op jit(solution)/shard_map/mix0/pallas_call | solution.py:564
  50.3 6.5 %attend1.1 = (bf16[2,16,2048,128]{3,2,1,0:T(8,128)(2,1)}, bf16[2,16,2048,128]{3,2,1,0:T(8,128)(2,1)}, bf16[16,2048,128]{2,1,0:T(8,128)(2,1)S(1)}, bf16[16,2048,1...) custom-call(s32[128]{0:T(128)S(1)} %copy-done, ...), custom_call_target="tpu_custom_call", output_to_operand_aliasing={{2}: (3, {}), {3}: (4, {}), {0}: (5, {}), {1}: (6, {})} | custom-call | tf_op jit(solution)/shard_map/attend1/pallas_call | solution.py:543
  56.9 26.1 %mix1.1 = bf16[128,4096]{1,0:T(8,128)(2,1)S(1)} custom-call(bf16[32,16,128]{2,1,0:T(8,128)(2,1)S(1)} %get-tuple-element.31.refs_0_, bf16[4,32,512]{2,1,0:T(8,128)(2,1)S(1)} %get-tuple-element.32.refs_1_, bf16[2,512,4096]{2,1,0:T(8,128)(2,1)} %refs_2_.3), custom_call_target="tpu_custom_call" | custom-call | tf_op jit(solution)/shard_map/mix1/pallas_call | solution.py:574
  83.0 1.0 %copy.24 = bf16[128,4096]{1,0:T(8,128)(2,1)} copy(bf16[128,4096]{1,0:T(8,128)(2,1)S(1)} %mix1.1) | data formatting | bytes 2097152
Async XLA Ops:
  0.6 9.4 %copy-start = (s32[128]{0:T(128)S(1)}, s32[128]{0:T(128)}, u32[]{:S(2)}) copy-start(s32[128]{0:T(128)} %refs_0_.3) | copy-start | bytes 1540

commit v9 on v8

--- a/solution.py
+++ b/solution.py
@@ -84,14 +84,19 @@
     return copies
 
 
-def cache_loads(layer, k_cache, v_cache, k_vmem, v_vmem, sems):
+def cut_of(seq_len):
+    return seq_len // 4 * 3
+
+
+def cache_loads(layer, k_cache, v_cache, k_vmem, v_vmem, sems, span):
     parts = sems.shape[0] // 2
     step = k_vmem.shape[0] // parts
     copies = []
     for i in range(parts):
         part = pl.ds(i * step, step)
-        copies.append(pltpu.make_async_copy(k_cache.at[layer, part], k_vmem.at[part], sems.at[2 * i]))
-        copies.append(pltpu.make_async_copy(v_cache.at[layer, part], v_vmem.at[part], sems.at[2 * i + 1]))
+        for n, (cache, buf) in enumerate(((k_cache, k_vmem), (v_cache, v_vmem))):
+            copies.append(pltpu.make_async_copy(
+                cache.at[layer, part, pl.ds(0, span)], buf.at[part, pl.ds(0, span)], sems.at[2 * i + n]))
     return copies
 
 
@@ -151,7 +156,7 @@
         pltpu.make_async_copy(x.at[:, pl.ds(i * depth, depth)], hidden.at[i], x_sems.at[i]) for i in range(pieces)
     ]
     w_copies = weight_copies(0, wq, wk, wv, wq_buf, wkv_buf, w_sems)
-    cache_copies = cache_loads(0, k_cache, v_cache, k_vmem, v_vmem, cache_sems)
+    cache_copies = cache_loads(0, k_cache, v_cache, k_vmem, v_vmem, cache_sems, cut_of(k_vmem.shape[1]))
     for i in range(pieces):
         x_copies[i].start()
         w_copies[i].start()
@@ -186,14 +191,14 @@
     context, residual, wo = take(3)
     if not last:
         wq, wk, wv, k_cache, v_cache = take(5)
-        q_out, kv_new, next_residual, k_vmem, v_vmem = take(5)
+        q_out, kv_new, next_residual, k_vmem, v_vmem, k_rest, v_rest = take(7)
     else:
         (hidden,) = take(1)
     c_recv, wo_far, wo_own, p_send, p_recv, total, s1_recv, comb, s2_left, s2_right = take(10)
     wo_sems, c_ssem, c_rsem, p_ssem, p_rsem, s1_ssem, s1_rsem = take(7)
     s2_ssem, s2_rsem, ag_ssem, ag_rsem, d2d_ssem, d2d_rsem = take(6)
     if not last:
-        hidden, wq_buf, wkv_buf, q_acc, q_send, w_sems, cache_sems, q_ssem, q_rsem = take(9)
+        hidden, wq_buf, wkv_buf, q_acc, q_send, w_sems, cache_sems, q_ssem, q_rsem, rest_sems = take(10)
     place = Place(count)
     heads, rows, head_dim = c_recv.shape
     local_rows = rows // count
@@ -212,7 +217,10 @@
         copy.start()
     if not last:
         w_copies = weight_copies(layer + 1, wq, wk, wv, wq_buf, wkv_buf, w_sems)
-        cache_copies = cache_loads(layer + 1, k_cache, v_cache, k_vmem, v_vmem, cache_sems)
+        cache_copies = cache_loads(layer + 1, k_cache, v_cache, k_vmem, v_vmem, cache_sems, k_vmem.shape[1])
+        cut, rest = cut_of(k_vmem.shape[1]), k_rest.shape[1]
+        for n, (cache, buf) in enumerate(((k_cache, k_rest), (v_cache, v_rest))):
+            cache_copies.append(pltpu.make_async_copy(cache.at[layer, :, pl.ds(cut, rest)], buf, rest_sems.at[n]))
         for copy in w_copies + cache_copies:
             copy.start()
 
@@ -386,39 +394,85 @@
 
 def attention_kernel(layer, *refs):
     all_lens, q, kv_new, k_in, v_in = refs[:5]
+    del k_in, v_in
     refs = refs[5:]
-    if layer > 0:
+    first = layer == 0
+    if first:
+        k_cache, v_cache = refs[:2]
         refs = refs[2:]
-    k_out, v_out, k_buf, v_buf, context, q_rows, c_rows, sems = refs
-    del k_in, v_in
+    else:
+        k_rest, v_rest = refs[2:4]
+        refs = refs[4:]
+    k_out, v_out, k_buf, v_buf, context, q_rows, c_rows, sems, load_sems, rest_sems = refs
     heads, local_rows, head_dim = q.shape
     seq_len = k_buf.shape[1]
+    cut = cut_of(seq_len)
+    rest = pl.ds(cut, seq_len - cut)
     tile = 16
     first_row = lax.axis_index("model") * local_rows
 
     def length(b):
         return all_lens[first_row + b]
 
+    def rest_loads(b):
+        return [
+            pltpu.make_async_copy(cache.at[0, b, rest], buf.at[b, rest], load_sems.at[2 * b + n])
+            for n, (cache, buf) in enumerate(((k_cache, k_buf), (v_cache, v_buf)))
+        ]
+
+    def rest_writes(b):
+        pairs = ((k_buf, k_out), (v_buf, v_out)) if first else ((k_rest, k_out), (v_rest, v_out))
+        return [
+            pltpu.make_async_copy(buf.at[b, rest] if first else buf.at[b], out.at[0, b, rest], rest_sems.at[2 * b + n])
+            for n, (buf, out) in enumerate(pairs)
+        ]
+
+    def each_rest(action):
+        def one(b, _):
+            @pl.when(length(b) >= cut if first else length(b) < cut)
+            def _():
+                action(b)
+            return 0
+        lax.fori_loop(0, local_rows, one, 0)
+
+    def write_token(b):
+        start = pl.multiple_of((length(b) // tile) * tile, tile)
+        here = lax.broadcasted_iota(jnp.int32, (tile, head_dim), 0) == length(b) - start
+        for buf, column in ((k_buf, 0), (v_buf, head_dim)):
+            fresh = jnp.broadcast_to(kv_new[b:b + 1, column:column + head_dim], (tile, head_dim))
+            old = buf[b, pl.ds(start, tile), :].astype(F32)
+            buf[b, pl.ds(start, tile), :] = jnp.where(here, fresh, old).astype(BF16)
+
+    def start_all(copies):
+        for copy in copies:
+            copy.start()
+
+    def wait_copies(copies):
+        for copy in copies:
+            copy.wait()
+
+    if first:
+        each_rest(lambda b: start_all(rest_loads(b)))
+    written = cut if first else seq_len
     writes = []
     parts = sems.shape[0] // 2
     step = local_rows // parts
     for i in range(parts):
         for b in range(i * step, (i + 1) * step):
-            start = pl.multiple_of((length(b) // tile) * tile, tile)
-            here = lax.broadcasted_iota(jnp.int32, (tile, head_dim), 0) == length(b) - start
-            for buf, column in ((k_buf, 0), (v_buf, head_dim)):
-                fresh = jnp.broadcast_to(kv_new[b:b + 1, column:column + head_dim], (tile, head_dim))
-                old = buf[b, pl.ds(start, tile), :].astype(F32)
-                buf[b, pl.ds(start, tile), :] = jnp.where(here, fresh, old).astype(BF16)
+            if first:
+                pl.when(length(b) < cut)(functools.partial(write_token, b))
+            else:
+                write_token(b)
         part = pl.ds(i * step, step)
-        writes.append(pltpu.make_async_copy(k_buf.at[part], k_out.at[layer, part], sems.at[2 * i]))
-        writes.append(pltpu.make_async_copy(v_buf.at[part], v_out.at[layer, part], sems.at[2 * i + 1]))
+        for n, (buf, out) in enumerate(((k_buf, k_out), (v_buf, v_out))):
+            writes.append(pltpu.make_async_copy(
+                buf.at[part, pl.ds(0, written)], out.at[layer, part, pl.ds(0, written)], sems.at[2 * i + n]))
         if i > 0:
-            writes[2 * i - 2].start()
-            writes[2 * i - 1].start()
+            start_all(writes[2 * i - 2:2 * i])
     q_rows[...] = q[...].astype(F32).reshape(heads * local_rows, head_dim)
-    writes[-2].start()
-    writes[-1].start()
+    start_all(writes[-2:])
+    if not first:
+        each_rest(lambda b: start_all(rest_writes(b)))
 
     def attend(members, span):
         rows = [pl.ds(b, heads, stride=local_rows) for b in members]
@@ -440,15 +494,23 @@
         for r, out in zip(rows, outs):
             c_rows[r, :] = out.astype(BF16).astype(F32)
 
-    for first in range(0, local_rows, GROUP):
-        attend(list(range(first, first + GROUP)), SHORT)
+    for base in range(0, local_rows, GROUP):
+        attend(list(range(base, base + GROUP)), SHORT)
+
+    if first:
+        for b in range(local_rows):
+            @pl.when(length(b) >= cut)
+            def _(b=b):
+                wait_copies(rest_loads(b))
+                write_token(b)
+        each_rest(lambda b: start_all(rest_writes(b)))
 
     spans = []
     span = 2 * SHORT
-    while span < seq_len:
+    while span < cut:
         spans.append(span)
         span *= 2
-    spans.append(seq_len)
+    spans += [cut, seq_len]
 
     def longer(b, _):
         @pl.when(length(b) >= SHORT)
@@ -463,8 +525,8 @@
 
     lax.fori_loop(0, local_rows, longer, 0)
     context[...] = c_rows[...].reshape(heads, local_rows, head_dim).astype(BF16)
-    for copy in writes:
-        copy.wait()
+    each_rest(lambda b: wait_copies(rest_writes(b)))
+    wait_copies(writes)
 
 
 def solution(mesh):
@@ -483,6 +545,7 @@
         pieces = 2 * CHUNKS
         depth = width // pieces
         chip_rows = rows // CHIPS
+        rest_shape = (local_rows, seq_len - cut_of(seq_len), head_dim)
         w_query, w_key, w_value, w_out = map(to_hbm, (w_query, w_key, w_value, w_out))
         x, k_cache, v_cache = map(to_hbm, (x, k_cache, v_cache))
 
@@ -537,9 +600,12 @@
             specs = [SMEM_SPEC] + [VMEM_SPEC] * 4
             aliases = {3: 2, 4: 3}
             if layer > 0:
-                operands += [k_new_cache, v_new_cache]
+                operands += [k_new_cache, v_new_cache, k_rest, v_rest]
+                specs += [ANY_SPEC] * 2 + [VMEM_SPEC] * 2
+                aliases |= {5: 0, 6: 1}
+            else:
+                operands += [k_cache, v_cache]
                 specs += [ANY_SPEC] * 2
-                aliases |= {5: 0, 6: 1}
             k_new_cache, v_new_cache, _, _, context = pl.pallas_call(
                 functools.partial(attention_kernel, layer),
                 out_shape=(
@@ -556,17 +622,19 @@
                     pltpu.VMEM((heads * local_rows, head_dim), F32),
                     pltpu.VMEM((heads * local_rows, head_dim), F32),
                     DMA((2 * PARTS,)),
+                    DMA((2 * local_rows,)),
+                    DMA((2 * local_rows,)),
                 ],
                 compiler_params=pltpu.CompilerParams(vmem_limit_bytes=16 * MIB),
                 name=f"attend{layer}",
             )(*operands)
             if not last:
-                query, kv_new, residual, k_vmem, v_vmem = pl.pallas_call(
+                query, kv_new, residual, k_vmem, v_vmem, k_rest, v_rest = pl.pallas_call(
                     functools.partial(mix_kernel, count, False, layer),
-                    out_shape=project_out,
+                    out_shape=project_out + (pltpu.VMEM(rest_shape, BF16),) * 2,
                     in_specs=[VMEM_SPEC] * 2 + [ANY_SPEC] * 6,
-                    out_specs=(VMEM_SPEC,) * 5,
-                    scratch_shapes=mix_scratch + project_scratch + project_sems,
+                    out_specs=(VMEM_SPEC,) * 7,
+                    scratch_shapes=mix_scratch + project_scratch + project_sems + [DMA((2,))],
                     compiler_params=params(1 + layer, 28),
                     name=f"mix{layer}",
                 )(context, residual, w_out, w_query, w_key, w_value, k_cache, v_cache)

time: 84.1 us -> 85.3 us (1.014)
  Pallas kernels: 82.3 us -> 83.5 us
    pallas_call x2, Pallas kernels: 13.1 us -> 14.4 us  [device_step(): pl.pallas_call(functools.partial(attention_kernel, layer), out_shape=(plt...]
where the time goes in v9:
time: 85.3 us; the launch traced here: 85.1 us
  Pallas kernels  83.5 us (98%)
  local copies, waits for them, and re-layouts  0.98 us (1%)
    pallas_call x1, Pallas kernels, device_step(): pl.pallas_call(functools.partial(mix_kernel, count, False, layer), out_sh...  33 us
    pallas_call x1, Pallas kernels, device_step(): pl.pallas_call(functools.partial(mix_kernel, count, True, layer), out_sha...  26.6 us
    pallas_call x2, Pallas kernels, device_step(): pl.pallas_call(functools.partial(attention_kernel, layer), out_shape=(plt...  14.4 us
    pallas_call x1, Pallas kernels, device_step(): pl.pallas_call(functools.partial(first_kernel, count), out_shape=project_...  9.36 us

profile of v9, /device:TPU:113, one launch (start us, length us, event | category | flops | bytes accessed | tf_op | source)
XLA Modules:
  0.0 85.1 jit_solution(3838943334384194109)
XLA Ops:
  0.6 0.0 copy-start
  0.6 9.4 %first.1 = (bf16[32,16,128]{2,1,0:T(8,128)(2,1)S(1)}, f32[16,256]{1,0:T(8,128)S(1)}, bf16[4,32,512]{2,1,0:T(8,128)(2,1)S(1)}, bf16[16,2048,128]{2,1,0:T(8,128)(2,1)S(1)}, bf16[16,2048,128]{2,1,0:T(8,128)(2,1)S(1)}) custom-call(bf16[128,4096]{1,0:T(8,128)(2,1)} %x.1, bf16[2,4096,512]{2,1,0:T(8,128)(2,1)} %refs_3_.1, bf16[2,4096,128]{2,1,0:T(8,128)(2,1)} %refs_4_.1, ...), custom_call_target="tpu_custom_call" | custom-call | tf_op jit(solution)/shard_map/first/pallas_call | solution.py:586
  10.0 0.0 copy-done
  10.0 6.2 %attend0.1 = (bf16[2,16,2048,128]{3,2,1,0:T(8,128)(2,1)}, bf16[2,16,2048,128]{3,2,1,0:T(8,128)(2,1)}, bf16[16,2048,128]{2,1,0:T(8,128)(2,1)S(1)}, bf16[16,2048,1...) custom-call(s32[128]{0:T(128)S(1)} %copy-done, ...), custom_call_target="tpu_custom_call", output_to_operand_aliasing={{2}: (3, {}), {3}: (4, {})} | custom-call | tf_op jit(solution)/shard_map/attend0/pallas_call | solution.py:609
  16.2 33.0 %mix0.1 = (bf16[32,16,128]{2,1,0:T(8,128)(2,1)S(1)}, f32[16,256]{1,0:T(8,128)S(1)}, bf16[4,32,512]{2,1,0:T(8,128)(2,1)S(1)}, bf16[16,2048,128]{2,1,0:T(8,128)(2,...) custom-call(bf16[32,16,128]{2,1,0:T(8,128)(2,1)S(1)} %get-tuple-elem, ...), custom_call_target="tpu_custom_call" | custom-call | tf_op jit(solution)/shard_map/mix0/pallas_call | solution.py:632
  49.2 8.3 %attend1.1 = (bf16[2,16,2048,128]{3,2,1,0:T(8,128)(2,1)}, bf16[2,16,2048,128]{3,2,1,0:T(8,128)(2,1)}, bf16[16,2048,128]{2,1,0:T(8,128)(2,1)S(1)}, bf16[16,2048,1...) custom-call(s32[128]{0:T(128)S(1)} %copy-done, ...), custom_call_target="tpu_custom_call", output_to_operand_aliasing={{2}: (3, {}), {3}: (4, {}), {0}: (5, {}), {1}: (6, {})} | custom-call | tf_op jit(solution)/shard_map/attend1/pallas_call | solution.py:609
  57.5 26.6 %mix1.1 = bf16[128,4096]{1,0:T(8,128)(2,1)S(1)} custom-call(bf16[32,16,128]{2,1,0:T(8,128)(2,1)S(1)} %get-tuple-element.35.refs_0_, bf16[4,32,512]{2,1,0:T(8,128)(2,1)S(1)} %get-tuple-element.36.refs_1_, bf16[2,512,4096]{2,1,0:T(8,128)(2,1)} %refs_2_.3), custom_call_target="tpu_custom_call" | custom-call | tf_op jit(solution)/shard_map/mix1/pallas_call | solution.py:642
  84.2 1.0 %copy.24 = bf16[128,4096]{1,0:T(8,128)(2,1)} copy(bf16[128,4096]{1,0:T(8,128)(2,1)S(1)} %mix1.1) | data formatting | bytes 2097152
Async XLA Ops:
  0.6 9.4 %copy-start = (s32[128]{0:T(128)S(1)}, s32[128]{0:T(128)}, u32[]{:S(2)}) copy-start(s32[128]{0:T(128)} %refs_0_.3) | copy-start | bytes 1540

commit v10 on v8

--- a/solution.py
+++ b/solution.py
@@ -14,7 +14,7 @@
 CHUNKS = 4
 PARTS = 8
 RING = 2
-RELAYED = 4
+EARLY = 2
 MIB = 1 << 20
 
 ANY_SPEC = pl.BlockSpec(memory_space=pltpu.HBM)
@@ -32,6 +32,10 @@
 
 def aligned(index, size):
     return pl.ds(pl.multiple_of(index * size, size), size)
+
+
+OWN, LEFT, RIGHT, ACROSS = range(4)
+MIRROR = (OWN, RIGHT, LEFT, ACROSS)
 
 
 class Place:
@@ -47,6 +51,10 @@
         self.to_right = self.right * 2 + 1 - self.core
         self.to_left = self.left * 2 + 1 - self.core
         self.sibling = self.chip * 2 + (1 - self.core)
+
+    def device(self, kind, cross):
+        chip = (self.chip, self.left, self.right, self.across)[kind]
+        return chip * 2 + (1 - self.core if cross else self.core)
 
     def peer(self, offset):
         return (self.me + offset) % self.count
@@ -216,14 +224,24 @@
         for copy in w_copies + cache_copies:
             copy.start()
 
-    c_recv[:, aligned(place.me, local_rows), :] = context[pl.ds(place.me * heads, heads)]
+    near = pl.ds(0, ACROSS * chip_rows)
+
+    def block(kind):
+        return pl.ds(kind * chip_rows, chip_rows)
+
+    def context_rows(kind, core):
+        return pl.ds(pl.multiple_of(kind * chip_rows + core * local_rows, local_rows), local_rows)
+
+    c_recv[:, context_rows(OWN, place.core), :] = context[pl.ds(place.me * heads, heads)]
     wait_all(place)
 
-    def context_copy(offset, source):
-        target = place.peer(offset)
+    def context_copy(kind, cross, incoming):
+        target = place.device(kind, cross)
+        sender = (1 - place.core if cross else place.core) if incoming else place.core
+        seen = kind if incoming else MIRROR[kind]
         return remote(
-            context.at[pl.ds(target * heads, heads)], c_recv.at[:, aligned(source, local_rows), :],
-            c_ssem.at[offset], c_rsem.at[offset], target)
+            context.at[pl.ds(target * heads, heads)], c_recv.at[:, context_rows(seen, sender), :],
+            c_ssem.at[2 * kind + cross], c_rsem.at[2 * seen + cross], target)
 
     sends = []
 
@@ -231,35 +249,44 @@
         copy.start()
         sends.append(copy)
 
-    for offset in send_order(count):
-        send(context_copy(offset, place.me))
-    for offset in range(1, count):
-        context_copy(offset, place.origin(offset)).wait_recv()
-
-    def product(weights):
+    for kind in (ACROSS, RIGHT, LEFT):
+        for cross in range(2):
+            send(context_copy(kind, cross, False))
+    send(context_copy(OWN, 1, False))
+
+    def product(weights, rows_of):
         acc = None
         for pair in range(heads // 2):
-            lhs = jnp.concatenate([c_recv[2 * pair], c_recv[2 * pair + 1]], axis=1)
+            lhs = jnp.concatenate([c_recv[2 * pair, rows_of], c_recv[2 * pair + 1, rows_of]], axis=1)
             part = jnp.dot(lhs, weights[pl.ds(pair * 2 * head_dim, 2 * head_dim), :], preferred_element_type=F32)
             acc = part if acc is None else acc + part
         return acc
 
-    def pair_copy(j):
-        return remote(p_send.at[j], p_recv.at[j], p_ssem.at[j], p_rsem.at[j], place.sibling)
-
-    def block(chip):
-        return aligned(chip, chip_rows)
-
+    def pair_copy(j, far):
+        part = block(ACROSS) if far else near
+        slot = far * CHUNKS + j
+        return remote(p_send.at[j, part], p_recv.at[j, part], p_ssem.at[slot], p_rsem.at[slot], place.sibling)
+
+    context_copy(OWN, 1, True).wait_recv()
+    for kind in (LEFT, RIGHT):
+        for cross in range(2):
+            context_copy(kind, cross, True).wait_recv()
     for j in range(CHUNKS):
         wo_copies[j].wait()
-        p_send[j] = product(wo_far.at[j])
-        send(pair_copy(j))
+        p_send[j, near] = product(wo_far.at[j], near)
+        send(pair_copy(j, 0))
+    for j in range(CHUNKS):
+        wo_copies[CHUNKS + j].wait()
+        total[j, near] = product(wo_own.at[j], near)
+    for cross in range(2):
+        context_copy(ACROSS, cross, True).wait_recv()
+    for j in range(CHUNKS):
+        p_send[j, block(ACROSS)] = product(wo_far.at[j], block(ACROSS))
+        send(pair_copy(j, 1))
 
     def step_one(j):
         target = place.to_right if j % 2 == 0 else place.to_left
-        if j >= RELAYED:
-            target = place.across * 2 + place.core
-        return remote(total.at[j, block(place.across), :], s1_recv.at[j], s1_ssem.at[j], s1_rsem.at[j], target)
+        return remote(total.at[j, block(ACROSS)], s1_recv.at[j], s1_ssem.at[j], s1_rsem.at[j], target)
 
     def step_two(j, rightward, source):
         target = place.to_right if rightward else place.to_left
@@ -268,43 +295,41 @@
         return remote(source, inbox.at[j], s2_ssem.at[slot], s2_rsem.at[slot], target)
 
     def direct(j):
-        for rightward in (j % 2 == 1, j % 2 == 0) if j >= RELAYED else (j % 2 == 1,):
-            send(step_two(j, rightward, total.at[j, block(place.right if rightward else place.left), :]))
+        rightward = j % 2 == 1
+        send(step_two(j, rightward, total.at[j, block(RIGHT if rightward else LEFT)]))
 
     def combine(j):
         step_one(j).wait_recv()
         rightward = j % 2 == 0
-        comb[j] = total[j, block(place.right if rightward else place.left), :] + s1_recv[j]
+        comb[j] = total[j, block(RIGHT if rightward else LEFT)] + s1_recv[j]
         send(step_two(j, rightward, comb.at[j]))
 
     for j in range(CHUNKS):
-        wo_copies[CHUNKS + j].wait()
-        total[j] = product(wo_own.at[j])
-    pending = []
-    for j in range(CHUNKS):
-        pair_copy(j).wait_recv()
-        total[j] += p_recv[j]
+        pair_copy(j, 0).wait_recv()
+        total[j, near] += p_recv[j, near]
+        if j < EARLY:
+            direct(j)
+    for j in range(CHUNKS):
+        total[j, block(ACROSS)] = product(wo_own.at[j], block(ACROSS))
+    for j in range(CHUNKS):
+        pair_copy(j, 1).wait_recv()
+        total[j, block(ACROSS)] += p_recv[j, block(ACROSS)]
         send(step_one(j))
-        while pending:
-            direct(pending.pop())
-        if 0 < j < RELAYED:
-            pending.append(j)
-        else:
-            direct(j)
-    for j in range(min(RELAYED, 2)):
+    for j in range(EARLY, CHUNKS):
+        direct(j)
+    for j in range(CHUNKS):
         combine(j)
-    while pending:
-        direct(pending.pop())
-    for j in range(2, RELAYED):
-        combine(j)
+
+    def chip_block(chip):
+        return aligned(chip, chip_rows)
 
     def piece(half, j):
         return half * CHUNKS + j
 
     def region(half, j, chip):
         if last:
-            return hidden.at[block(chip), aligned(piece(half, j), depth)]
-        return hidden.at[piece(half, j), block(chip), :]
+            return hidden.at[chip_block(chip), aligned(piece(half, j), depth)]
+        return hidden.at[piece(half, j), chip_block(chip), :]
 
     def gather_copy(j, way, chip):
         target = (place.to_right, place.to_left, place.across * 2 + place.core)[way]
@@ -324,15 +349,12 @@
     def finish(j):
         step_two(j, True, comb.at[j]).wait_recv()
         step_two(j, False, comb.at[j]).wait_recv()
-        summed = total[j, block(place.chip), :] + s2_left[j] + s2_right[j]
-        if j >= RELAYED:
-            step_one(j).wait_recv()
-            summed = summed + s1_recv[j]
+        summed = total[j, block(OWN)] + s2_left[j] + s2_right[j]
         value = (residual[j].astype(F32) + summed).astype(BF16)
         if last:
-            hidden[block(place.chip), aligned(piece(place.half, j), depth)] = value
+            hidden[chip_block(place.chip), aligned(piece(place.half, j), depth)] = value
         else:
-            hidden[piece(place.half, j), block(place.chip), :] = value
+            hidden[piece(place.half, j), chip_block(place.chip), :] = value
             next_residual[j] = value
         if j >= RING:
             send(gather_copy(j, 2, place.chip))
@@ -512,7 +534,7 @@
             pltpu.VMEM((CHUNKS, chip_rows, depth), F32),
             pltpu.VMEM((CHUNKS, chip_rows, depth), F32),
             pltpu.VMEM((CHUNKS, chip_rows, depth), F32),
-            DMA((pieces,)), DMA((count,)), DMA((count,)), DMA((CHUNKS,)), DMA((CHUNKS,)), DMA((CHUNKS,)), DMA((CHUNKS,)),
+            DMA((pieces,)), DMA((count,)), DMA((count,)), DMA((pieces,)), DMA((pieces,)), DMA((CHUNKS,)), DMA((CHUNKS,)),
             DMA((2 * CHUNKS,)), DMA((2 * CHUNKS,)), DMA((3 * CHUNKS,)), DMA((3 * CHUNKS,)),
             DMA((CHUNKS,)), DMA((CHUNKS,)),
         ]

time: 84.1 us -> 86.7 us (1.031)
  Pallas kernels: 82.3 us -> 85 us
    pallas_call x1, Pallas kernels: 33.8 us -> 35.6 us  [device_step(): pl.pallas_call(functools.partial(mix_kernel, count, False, layer), out_sh...]
where the time goes in v10:
time: 86.7 us; the launch traced here: 86.6 us
  Pallas kernels  85 us (98%)
  local copies, waits for them, and re-layouts  0.98 us (1%)
    pallas_call x1, Pallas kernels, device_step(): pl.pallas_call(functools.partial(mix_kernel, count, False, layer), out_sh...  35.6 us
    pallas_call x1, Pallas kernels, device_step(): pl.pallas_call(functools.partial(mix_kernel, count, True, layer), out_sha...  26.9 us
    pallas_call x2, Pallas kernels, device_step(): pl.pallas_call(functools.partial(attention_kernel, layer), out_shape=(plt...  13.1 us
    pallas_call x1, Pallas kernels, device_step(): pl.pallas_call(functools.partial(first_kernel, count), out_shape=project_...  9.36 us

profile of v10, /device:TPU:113, one launch (start us, length us, event | category | flops | bytes accessed | tf_op | source)
XLA Modules:
  0.0 86.6 jit_solution(12233992239316903087)
XLA Ops:
  0.6 0.0 copy-start
  0.6 9.4 %first.1 = (bf16[32,16,128]{2,1,0:T(8,128)(2,1)S(1)}, f32[16,256]{1,0:T(8,128)S(1)}, bf16[4,32,512]{2,1,0:T(8,128)(2,1)S(1)}, bf16[16,2048,128]{2,1,0:T(8,128)(2,1)S(1)}, bf16[16,2048,128]{2,1,0:T(8,128)(2,1)S(1)}) custom-call(bf16[128,4096]{1,0:T(8,128)(2,1)} %x.1, bf16[2,4096,512]{2,1,0:T(8,128)(2,1)} %refs_3_.1, bf16[2,4096,128]{2,1,0:T(8,128)(2,1)} %refs_4_.1, ...), custom_call_target="tpu_custom_call" | custom-call | tf_op jit(solution)/shard_map/first/pallas_call | solution.py:545
  10.0 0.0 copy-done
  10.0 6.5 %attend0.1 = (bf16[2,16,2048,128]{3,2,1,0:T(8,128)(2,1)}, bf16[2,16,2048,128]{3,2,1,0:T(8,128)(2,1)}, bf16[16,2048,128]{2,1,0:T(8,128)(2,1)S(1)}, bf16[16,2048,1...) custom-call(s32[128]{0:T(128)S(1)} %copy-done, ...), custom_call_target="tpu_custom_call", output_to_operand_aliasing={{2}: (3, {}), {3}: (4, {})} | custom-call | tf_op jit(solution)/shard_map/attend0/pallas_call | solution.py:565
  16.6 35.6 %mix0.1 = (bf16[32,16,128]{2,1,0:T(8,128)(2,1)S(1)}, f32[16,256]{1,0:T(8,128)S(1)}, bf16[4,32,512]{2,1,0:T(8,128)(2,1)S(1)}, bf16[16,2048,128]{2,1,0:T(8,128)(2,1)S(1)}, bf16[16,2048,128]{2,1,0:T(8,128)(2,1)S(1)}) custom-call(bf16[32,16,128]{2,1,0:T(8,128)(2,1)S(1)} %get-tuple-element.23.refs_0_, bf16[4,32,512]{2,1,0:T(8,128)(2,1)S(1)} %get-tuple-element.24.refs_1_, ...), custom_call_target="tpu_custom_call" | custom-call | tf_op jit(solution)/shard_map/mix0/pallas_call | solution.py:586
  52.1 6.5 %attend1.1 = (bf16[2,16,2048,128]{3,2,1,0:T(8,128)(2,1)}, bf16[2,16,2048,128]{3,2,1,0:T(8,128)(2,1)}, bf16[16,2048,128]{2,1,0:T(8,128)(2,1)S(1)}, bf16[16,2048,1...) custom-call(s32[128]{0:T(128)S(1)} %copy-done, ...), custom_call_target="tpu_custom_call", output_to_operand_aliasing={{2}: (3, {}), {3}: (4, {}), {0}: (5, {}), {1}: (6, {})} | custom-call | tf_op jit(solution)/shard_map/attend1/pallas_call | solution.py:565
  58.7 26.9 %mix1.1 = bf16[128,4096]{1,0:T(8,128)(2,1)S(1)} custom-call(bf16[32,16,128]{2,1,0:T(8,128)(2,1)S(1)} %get-tuple-element.31.refs_0_, bf16[4,32,512]{2,1,0:T(8,128)(2,1)S(1)} %get-tuple-element.32.refs_1_, bf16[2,512,4096]{2,1,0:T(8,128)(2,1)} %refs_2_.3), custom_call_target="tpu_custom_call" | custom-call | tf_op jit(solution)/shard_map/mix1/pallas_call | solution.py:596
  85.6 1.0 %copy.24 = bf16[128,4096]{1,0:T(8,128)(2,1)} copy(bf16[128,4096]{1,0:T(8,128)(2,1)S(1)} %mix1.1) | data formatting | bytes 2097152
Async XLA Ops:
  0.6 9.4 %copy-start = (s32[128]{0:T(128)S(1)}, s32[128]{0:T(128)}, u32[]{:S(2)}) copy-start(s32[128]{0:T(128)} %refs_0_.3) | copy-start | bytes 1540

commit v11 on v8

--- a/solution.py
+++ b/solution.py
@@ -13,7 +13,7 @@
 CHIPS = 4
 CHUNKS = 4
 PARTS = 8
-RING = 2
+RING = 4
 RELAYED = 4
 MIB = 1 << 20
 

time: 84.1 us -> 85 us (1.011)
  Pallas kernels: 82.3 us -> 83.2 us
    pallas_call x1, Pallas kernels: 33.8 us -> 34.9 us  [device_step(): pl.pallas_call(functools.partial(mix_kernel, count, False, layer), out_sh...]
where the time goes in v11:
time: 85 us; the launch traced here: 84.9 us
  Pallas kernels  83.2 us (98%)
  local copies, waits for them, and re-layouts  0.98 us (1%)
    pallas_call x1, Pallas kernels, device_step(): pl.pallas_call(functools.partial(mix_kernel, count, False, layer), out_sh...  34.9 us
    pallas_call x1, Pallas kernels, device_step(): pl.pallas_call(functools.partial(mix_kernel, count, True, layer), out_sha...  25.9 us
    pallas_call x2, Pallas kernels, device_step(): pl.pallas_call(functools.partial(attention_kernel, layer), out_shape=(plt...  13.1 us
    pallas_call x1, Pallas kernels, device_step(): pl.pallas_call(functools.partial(first_kernel, count), out_shape=project_...  9.36 us

profile of v11, /device:TPU:113, one launch (start us, length us, event | category | flops | bytes accessed | tf_op | source)
XLA Modules:
  0.0 84.9 jit_solution(12920540426967172591)
XLA Ops:
  0.6 0.0 copy-start
  0.6 9.4 %first.1 = (bf16[32,16,128]{2,1,0:T(8,128)(2,1)S(1)}, f32[16,256]{1,0:T(8,128)S(1)}, bf16[4,32,512]{2,1,0:T(8,128)(2,1)S(1)}, bf16[16,2048,128]{2,1,0:T(8,128)(2,1)S(1)}, bf16[16,2048,128]{2,1,0:T(8,128)(2,1)S(1)}) custom-call(bf16[128,4096]{1,0:T(8,128)(2,1)} %x.1, bf16[2,4096,512]{2,1,0:T(8,128)(2,1)} %refs_3_.1, bf16[2,4096,128]{2,1,0:T(8,128)(2,1)} %refs_4_.1, ...), custom_call_target="tpu_custom_call" | custom-call | tf_op jit(solution)/shard_map/first/pallas_call | solution.py:523
  10.0 0.0 copy-done
  10.0 6.5 %attend0.1 = (bf16[2,16,2048,128]{3,2,1,0:T(8,128)(2,1)}, bf16[2,16,2048,128]{3,2,1,0:T(8,128)(2,1)}, bf16[16,2048,128]{2,1,0:T(8,128)(2,1)S(1)}, bf16[16,2048,1...) custom-call(s32[128]{0:T(128)S(1)} %copy-done, ...), custom_call_target="tpu_custom_call", output_to_operand_aliasing={{2}: (3, {}), {3}: (4, {})} | custom-call | tf_op jit(solution)/shard_map/attend0/pallas_call | solution.py:543
  16.6 34.9 %mix0.1 = (bf16[32,16,128]{2,1,0:T(8,128)(2,1)S(1)}, f32[16,256]{1,0:T(8,128)S(1)}, bf16[4,32,512]{2,1,0:T(8,128)(2,1)S(1)}, bf16[16,2048,128]{2,1,0:T(8,128)(2,1)S(1)}, bf16[16,2048,128]{2,1,0:T(8,128)(2,1)S(1)}) custom-call(bf16[32,16,128]{2,1,0:T(8,128)(2,1)S(1)} %get-tuple-element.23.refs_0_, bf16[4,32,512]{2,1,0:T(8,128)(2,1)S(1)} %get-tuple-element.24.refs_1_, ...), custom_call_target="tpu_custom_call" | custom-call | tf_op jit(solution)/shard_map/mix0/pallas_call | solution.py:564
  51.5 6.5 %attend1.1 = (bf16[2,16,2048,128]{3,2,1,0:T(8,128)(2,1)}, bf16[2,16,2048,128]{3,2,1,0:T(8,128)(2,1)}, bf16[16,2048,128]{2,1,0:T(8,128)(2,1)S(1)}, bf16[16,2048,1...) custom-call(s32[128]{0:T(128)S(1)} %copy-done, ...), custom_call_target="tpu_custom_call", output_to_operand_aliasing={{2}: (3, {}), {3}: (4, {}), {0}: (5, {}), {1}: (6, {})} | custom-call | tf_op jit(solution)/shard_map/attend1/pallas_call | solution.py:543
  58.0 25.9 %mix1.1 = bf16[128,4096]{1,0:T(8,128)(2,1)S(1)} custom-call(bf16[32,16,128]{2,1,0:T(8,128)(2,1)S(1)} %get-tuple-element.31.refs_0_, bf16[4,32,512]{2,1,0:T(8,128)(2,1)S(1)} %get-tuple-element.32.refs_1_, bf16[2,512,4096]{2,1,0:T(8,128)(2,1)} %refs_2_.3), custom_call_target="tpu_custom_call" | custom-call | tf_op jit(solution)/shard_map/mix1/pallas_call | solution.py:574
  83.9 1.0 %copy.24 = bf16[128,4096]{1,0:T(8,128)(2,1)} copy(bf16[128,4096]{1,0:T(8,128)(2,1)S(1)} %mix1.1) | data formatting | bytes 2097152
Async XLA Ops:
  0.6 9.4 %copy-start = (s32[128]{0:T(128)S(1)}, s32[128]{0:T(128)}, u32[]{:S(2)}) copy-start(s32[128]{0:T(128)} %refs_0_.3) | copy-start | bytes 1540

commit v12 on v11

--- a/solution.py
+++ b/solution.py
@@ -13,7 +13,7 @@
 CHIPS = 4
 CHUNKS = 4
 PARTS = 8
-RING = 4
+RING = 0
 RELAYED = 4
 MIB = 1 << 20
 

time: 85 us -> 83.8 us (0.986)
  Pallas kernels: 83.2 us -> 82.1 us
    pallas_call x1, Pallas kernels: 34.9 us -> 32.9 us  [device_step(): pl.pallas_call(functools.partial(mix_kernel, count, False, layer), out_sh...]
where the time goes in v12:
time: 83.8 us; the launch traced here: 83.7 us
  Pallas kernels  82.1 us (98%)
  local copies, waits for them, and re-layouts  0.98 us (1%)
    pallas_call x1, Pallas kernels, device_step(): pl.pallas_call(functools.partial(mix_kernel, count, False, layer), out_sh...  32.9 us
    pallas_call x1, Pallas kernels, device_step(): pl.pallas_call(functools.partial(mix_kernel, count, True, layer), out_sha...  26.7 us
    pallas_call x2, Pallas kernels, device_step(): pl.pallas_call(functools.partial(attention_kernel, layer), out_shape=(plt...  13.1 us
    pallas_call x1, Pallas kernels, device_step(): pl.pallas_call(functools.partial(first_kernel, count), out_shape=project_...  9.36 us

profile of v12, /device:TPU:113, one launch (start us, length us, event | category | flops | bytes accessed | tf_op | source)
XLA Modules:
  0.0 83.7 jit_solution(14200599752666619294)
XLA Ops:
  0.6 0.0 copy-start
  0.6 9.4 %first.1 = (bf16[32,16,128]{2,1,0:T(8,128)(2,1)S(1)}, f32[16,256]{1,0:T(8,128)S(1)}, bf16[4,32,512]{2,1,0:T(8,128)(2,1)S(1)}, bf16[16,2048,128]{2,1,0:T(8,128)(2,1)S(1)}, bf16[16,2048,128]{2,1,0:T(8,128)(2,1)S(1)}) custom-call(bf16[128,4096]{1,0:T(8,128)(2,1)} %x.1, bf16[2,4096,512]{2,1,0:T(8,128)(2,1)} %refs_3_.1, bf16[2,4096,128]{2,1,0:T(8,128)(2,1)} %refs_4_.1, ...), custom_call_target="tpu_custom_call" | custom-call | tf_op jit(solution)/shard_map/first/pallas_call | solution.py:523
  10.0 0.0 copy-done
  10.0 6.5 %attend0.1 = (bf16[2,16,2048,128]{3,2,1,0:T(8,128)(2,1)}, bf16[2,16,2048,128]{3,2,1,0:T(8,128)(2,1)}, bf16[16,2048,128]{2,1,0:T(8,128)(2,1)S(1)}, bf16[16,2048,1...) custom-call(s32[128]{0:T(128)S(1)} %copy-done, ...), custom_call_target="tpu_custom_call", output_to_operand_aliasing={{2}: (3, {}), {3}: (4, {})} | custom-call | tf_op jit(solution)/shard_map/attend0/pallas_call | solution.py:543
  16.6 32.9 %mix0.1 = (bf16[32,16,128]{2,1,0:T(8,128)(2,1)S(1)}, f32[16,256]{1,0:T(8,128)S(1)}, bf16[4,32,512]{2,1,0:T(8,128)(2,1)S(1)}, bf16[16,2048,128]{2,1,0:T(8,128)(2,1)S(1)}, bf16[16,2048,128]{2,1,0:T(8,128)(2,1)S(1)}) custom-call(bf16[32,16,128]{2,1,0:T(8,128)(2,1)S(1)} %get-tuple-element.23.refs_0_, bf16[4,32,512]{2,1,0:T(8,128)(2,1)S(1)} %get-tuple-element.24.refs_1_, ...), custom_call_target="tpu_custom_call" | custom-call | tf_op jit(solution)/shard_map/mix0/pallas_call | solution.py:564
  49.5 6.5 %attend1.1 = (bf16[2,16,2048,128]{3,2,1,0:T(8,128)(2,1)}, bf16[2,16,2048,128]{3,2,1,0:T(8,128)(2,1)}, bf16[16,2048,128]{2,1,0:T(8,128)(2,1)S(1)}, bf16[16,2048,1...) custom-call(s32[128]{0:T(128)S(1)} %copy-done, ...), custom_call_target="tpu_custom_call", output_to_operand_aliasing={{2}: (3, {}), {3}: (4, {}), {0}: (5, {}), {1}: (6, {})} | custom-call | tf_op jit(solution)/shard_map/attend1/pallas_call | solution.py:543
  56.1 26.7 %mix1.1 = bf16[128,4096]{1,0:T(8,128)(2,1)S(1)} custom-call(bf16[32,16,128]{2,1,0:T(8,128)(2,1)S(1)} %get-tuple-element.31.refs_0_, bf16[4,32,512]{2,1,0:T(8,128)(2,1)S(1)} %get-tuple-element.32.refs_1_, bf16[2,512,4096]{2,1,0:T(8,128)(2,1)} %refs_2_.3), custom_call_target="tpu_custom_call" | custom-call | tf_op jit(solution)/shard_map/mix1/pallas_call | solution.py:574
  82.8 1.0 %copy.24 = bf16[128,4096]{1,0:T(8,128)(2,1)} copy(bf16[128,4096]{1,0:T(8,128)(2,1)S(1)} %mix1.1) | data formatting | bytes 2097152
Async XLA Ops:
  0.6 9.4 %copy-start = (s32[128]{0:T(128)S(1)}, s32[128]{0:T(128)}, u32[]{:S(2)}) copy-start(s32[128]{0:T(128)} %refs_0_.3) | copy-start | bytes 1540

commit v13 on v12

--- a/solution.py
+++ b/solution.py
@@ -11,10 +11,10 @@
 F32 = jnp.float32
 BF16 = jnp.bfloat16
 CHIPS = 4
-CHUNKS = 4
+CHUNKS = 2
 PARTS = 8
 RING = 0
-RELAYED = 4
+RELAYED = CHUNKS
 MIB = 1 << 20
 
 ANY_SPEC = pl.BlockSpec(memory_space=pltpu.HBM)

time: 83.8 us -> 87.7 us (1.047)
  Pallas kernels: 82.1 us -> 85.9 us
    pallas_call x1, Pallas kernels: 32.9 us -> 35 us  [device_step(): pl.pallas_call(functools.partial(mix_kernel, count, False, layer), out_sh...]
    pallas_call x1, Pallas kernels: 26.7 us -> 28.5 us  [device_step(): pl.pallas_call(functools.partial(mix_kernel, count, True, layer), out_sha...]
where the time goes in v13:
time: 87.7 us; the launch traced here: 87.6 us
  Pallas kernels  85.9 us (98%)
  local copies, waits for them, and re-layouts  0.98 us (1%)
    pallas_call x1, Pallas kernels, device_step(): pl.pallas_call(functools.partial(mix_kernel, count, False, layer), out_sh...  35 us
    pallas_call x1, Pallas kernels, device_step(): pl.pallas_call(functools.partial(mix_kernel, count, True, layer), out_sha...  28.5 us
    pallas_call x2, Pallas kernels, device_step(): pl.pallas_call(functools.partial(attention_kernel, layer), out_shape=(plt...  13.1 us
    pallas_call x1, Pallas kernels, device_step(): pl.pallas_call(functools.partial(first_kernel, count), out_shape=project_...  9.37 us

profile of v13, /device:TPU:113, one launch (start us, length us, event | category | flops | bytes accessed | tf_op | source)
XLA Modules:
  0.0 87.6 jit_solution(14495285399306039964)
XLA Ops:
  0.6 0.0 copy-start
  0.6 9.4 %first.1 = (bf16[32,16,128]{2,1,0:T(8,128)(2,1)S(1)}, f32[16,256]{1,0:T(8,128)S(1)}, bf16[2,32,1024]{2,1,0:T(8,128)(2,1)S(1)}, bf16[16,2048,128]{2,1,0:T(8,128)(2,1)S(1)}, bf16[16,2048,128]{2,1,0:T(8,128)(2,1)S(1)}) custom-call(bf16[128,4096]{1,0:T(8,128)(2,1)} %x.1, bf16[2,4096,512]{2,1,0:T(8,128)(2,1)} %refs_3_.1, bf16[2,4096,128]{2,1,0:T(8,128)(2,1)} %refs_4_.1, ...), custom_call_target="tpu_custom_call" | custom-call | tf_op jit(solution)/shard_map/first/pallas_call | solution.py:523
  10.0 0.0 copy-done
  10.0 6.5 %attend0.1 = (bf16[2,16,2048,128]{3,2,1,0:T(8,128)(2,1)}, bf16[2,16,2048,128]{3,2,1,0:T(8,128)(2,1)}, bf16[16,2048,128]{2,1,0:T(8,128)(2,1)S(1)}, bf16[16,2048,1...) custom-call(s32[128]{0:T(128)S(1)} %copy-done, ...), custom_call_target="tpu_custom_call", output_to_operand_aliasing={{2}: (3, {}), {3}: (4, {})} | custom-call | tf_op jit(solution)/shard_map/attend0/pallas_call | solution.py:543
  16.6 35.0 %mix0.1 = (bf16[32,16,128]{2,1,0:T(8,128)(2,1)S(1)}, f32[16,256]{1,0:T(8,128)S(1)}, bf16[2,32,1024]{2,1,0:T(8,128)(2,1)S(1)}, bf16[16,2048,128]{2,1,0:T(8,128)(2,1)S(1)}, bf16[16,2048,128]{2,1,0:T(8,128)(2,1)S(1)}) custom-call(bf16[32,16,128]{2,1,0:T(8,128)(2,1)S(1)} %get-tuple-element.23.refs_0_, bf16[2,32,1024]{2,1,0:T(8,128)(2,1)S(1)} %get-tuple-element.24.refs_1_, ...), custom_call_target="tpu_custom_call" | custom-call | tf_op jit(solution)/shard_map/mix0/pallas_call | solution.py:564
  51.6 6.5 %attend1.1 = (bf16[2,16,2048,128]{3,2,1,0:T(8,128)(2,1)}, bf16[2,16,2048,128]{3,2,1,0:T(8,128)(2,1)}, bf16[16,2048,128]{2,1,0:T(8,128)(2,1)S(1)}, bf16[16,2048,1...) custom-call(s32[128]{0:T(128)S(1)} %copy-done, ...), custom_call_target="tpu_custom_call", output_to_operand_aliasing={{2}: (3, {}), {3}: (4, {}), {0}: (5, {}), {1}: (6, {})} | custom-call | tf_op jit(solution)/shard_map/attend1/pallas_call | solution.py:543
  58.1 28.5 %mix1.1 = bf16[128,4096]{1,0:T(8,128)(2,1)S(1)} custom-call(bf16[32,16,128]{2,1,0:T(8,128)(2,1)S(1)} %get-tuple-element.31.refs_0_, bf16[2,32,1024]{2,1,0:T(8,128)(2,1)S(1)} %get-tuple-element.32.refs_1_, bf16[2,512,4096]{2,1,0:T(8,128)(2,1)} %refs_2_.3), custom_call_target="tpu_custom_call" | custom-call | tf_op jit(solution)/shard_map/mix1/pallas_call | solution.py:574
  86.6 1.0 %copy.24 = bf16[128,4096]{1,0:T(8,128)(2,1)} copy(bf16[128,4096]{1,0:T(8,128)(2,1)S(1)} %mix1.1) | data formatting | bytes 2097152
Async XLA Ops:
  0.6 9.4 %copy-start = (s32[128]{0:T(128)S(1)}, s32[128]{0:T(128)}, u32[]{:S(2)}) copy-start(s32[128]{0:T(128)} %refs_0_.3) | copy-start | bytes 1540

commit v14 on v12

--- a/solution.py
+++ b/solution.py
@@ -291,11 +291,9 @@
             pending.append(j)
         else:
             direct(j)
-    for j in range(min(RELAYED, 2)):
-        combine(j)
     while pending:
         direct(pending.pop())
-    for j in range(2, RELAYED):
+    for j in range(RELAYED):
         combine(j)
 
     def piece(half, j):

time: 83.8 us -> 84.8 us (1.012)
  Pallas kernels: 82.1 us -> 83 us
    pallas_call x1, Pallas kernels: 32.9 us -> 33.8 us  [device_step(): pl.pallas_call(functools.partial(mix_kernel, count, False, layer), out_sh...]
where the time goes in v14:
time: 84.8 us; the launch traced here: 84.7 us
  Pallas kernels  83 us (98%)
  local copies, waits for them, and re-layouts  0.98 us (1%)
    pallas_call x1, Pallas kernels, device_step(): pl.pallas_call(functools.partial(mix_kernel, count, False, layer), out_sh...  33.8 us
    pallas_call x1, Pallas kernels, device_step(): pl.pallas_call(functools.partial(mix_kernel, count, True, layer), out_sha...  26.7 us
    pallas_call x2, Pallas kernels, device_step(): pl.pallas_call(functools.partial(attention_kernel, layer), out_shape=(plt...  13.1 us
    pallas_call x1, Pallas kernels, device_step(): pl.pallas_call(functools.partial(first_kernel, count), out_shape=project_...  9.36 us

profile of v14, /device:TPU:113, one launch (start us, length us, event | category | flops | bytes accessed | tf_op | source)
XLA Modules:
  0.0 84.7 jit_solution(10165858429096679881)
XLA Ops:
  0.6 0.0 copy-start
  0.6 9.4 %first.1 = (bf16[32,16,128]{2,1,0:T(8,128)(2,1)S(1)}, f32[16,256]{1,0:T(8,128)S(1)}, bf16[4,32,512]{2,1,0:T(8,128)(2,1)S(1)}, bf16[16,2048,128]{2,1,0:T(8,128)(2,1)S(1)}, bf16[16,2048,128]{2,1,0:T(8,128)(2,1)S(1)}) custom-call(bf16[128,4096]{1,0:T(8,128)(2,1)} %x.1, bf16[2,4096,512]{2,1,0:T(8,128)(2,1)} %refs_3_.1, bf16[2,4096,128]{2,1,0:T(8,128)(2,1)} %refs_4_.1, ...), custom_call_target="tpu_custom_call" | custom-call | tf_op jit(solution)/shard_map/first/pallas_call | solution.py:521
  10.0 0.0 copy-done
  10.0 6.5 %attend0.1 = (bf16[2,16,2048,128]{3,2,1,0:T(8,128)(2,1)}, bf16[2,16,2048,128]{3,2,1,0:T(8,128)(2,1)}, bf16[16,2048,128]{2,1,0:T(8,128)(2,1)S(1)}, bf16[16,2048,1...) custom-call(s32[128]{0:T(128)S(1)} %copy-done, ...), custom_call_target="tpu_custom_call", output_to_operand_aliasing={{2}: (3, {}), {3}: (4, {})} | custom-call | tf_op jit(solution)/shard_map/attend0/pallas_call | solution.py:541
  16.6 33.8 %mix0.1 = (bf16[32,16,128]{2,1,0:T(8,128)(2,1)S(1)}, f32[16,256]{1,0:T(8,128)S(1)}, bf16[4,32,512]{2,1,0:T(8,128)(2,1)S(1)}, bf16[16,2048,128]{2,1,0:T(8,128)(2,1)S(1)}, bf16[16,2048,128]{2,1,0:T(8,128)(2,1)S(1)}) custom-call(bf16[32,16,128]{2,1,0:T(8,128)(2,1)S(1)} %get-tuple-element.23.refs_0_, bf16[4,32,512]{2,1,0:T(8,128)(2,1)S(1)} %get-tuple-element.24.refs_1_, ...), custom_call_target="tpu_custom_call" | custom-call | tf_op jit(solution)/shard_map/mix0/pallas_call | solution.py:562
  50.4 6.5 %attend1.1 = (bf16[2,16,2048,128]{3,2,1,0:T(8,128)(2,1)}, bf16[2,16,2048,128]{3,2,1,0:T(8,128)(2,1)}, bf16[16,2048,128]{2,1,0:T(8,128)(2,1)S(1)}, bf16[16,2048,1...) custom-call(s32[128]{0:T(128)S(1)} %copy-done, ...), custom_call_target="tpu_custom_call", output_to_operand_aliasing={{2}: (3, {}), {3}: (4, {}), {0}: (5, {}), {1}: (6, {})} | custom-call | tf_op jit(solution)/shard_map/attend1/pallas_call | solution.py:541
  57.0 26.7 %mix1.1 = bf16[128,4096]{1,0:T(8,128)(2,1)S(1)} custom-call(bf16[32,16,128]{2,1,0:T(8,128)(2,1)S(1)} %get-tuple-element.31.refs_0_, bf16[4,32,512]{2,1,0:T(8,128)(2,1)S(1)} %get-tuple-element.32.refs_1_, bf16[2,512,4096]{2,1,0:T(8,128)(2,1)} %refs_2_.3), custom_call_target="tpu_custom_call" | custom-call | tf_op jit(solution)/shard_map/mix1/pallas_call | solution.py:572
  83.7 1.0 %copy.24 = bf16[128,4096]{1,0:T(8,128)(2,1)} copy(bf16[128,4096]{1,0:T(8,128)(2,1)S(1)} %mix1.1) | data formatting | bytes 2097152
Async XLA Ops:
  0.6 9.4 %copy-start = (s32[128]{0:T(128)S(1)}, s32[128]{0:T(128)}, u32[]{:S(2)}) copy-start(s32[128]{0:T(128)} %refs_0_.3) | copy-start | bytes 1540
